TPU v7x, 128 devices: a whole 4x4x4 slice. The times are simulated.
128 devices in a mesh: slab: 32 (over z, y, core), row: 4 (over x).
Axes of the slice: x: 4, y: 4, z: 4, core: 2. Of those that a mesh axis runs over, the one named last changes fastest.
Arguments:
- voltage: float32 [512, 98304], P(None, ('slab', 'row')), may hold values from -6 to 6
- potential: float32 [256, 512, 256], P('slab', 'row'), may hold values from -6 to 6
- transfer: float32 [128, 512], replicated, may hold values from -0.25 to 0.25
- conductance: float32 [512], replicated, may hold values from 0.2 to 2
- inverses: float32 [8, 64, 64], replicated, may hold values from -1 to 1
- parents: int32 [7], replicated, may hold values from 0 to 6, as said below
- target: int32 [98304, 1], P(('slab', 'row')), may hold values from 0 to 127; in each aligned block of 768 rows (0 to 767, 768 to 1535, ...) at most 12 rows name the same one
- place: int32 [98304], P(('slab', 'row')), may hold values from 0 to 2047
Outputs:
- voltage_out: float32 [512, 98304], P(None, ('slab', 'row'))
- potential_out: float32 [256, 512, 256], P('slab', 'row')
Inputs may be any that keep to these rules, and one draw needn't show every extreme that they name: `target`: among the 768 cells of one device, at most 12 name the same owner; in every draw some owner is named by exactly 12 of one device's cells. `parents`: entry k is smaller than k + 1; the last entry is 6.
All inputs are finite; a program needn't handle non-finite values.
Results may differ from a plain program's by a relative error of at most 0.00011.
Values sent between devices are 32-bit elements; how exact they have to be, the bound alone decides.
A program may use at most 64 MiB of HBM per device.

v0:
```python
import jax
import jax.numpy as jnp
from jax import lax
from jax.sharding import PartitionSpec as P

STEPS = 2
SWEEPS = 4


screening = 0.25
coupling = 0.5


def padded_2(block, sides, width):
    for axis, dim in sides:
        count = lax.axis_size(axis)
        forward = [(i, i + 1) for i in range(count - 1)]
        backward = [(target, source) for source, target in forward]
        low = lax.ppermute(
            lax.slice_in_dim(block, block.shape[dim] - width, None, axis=dim), axis, forward
        )
        high = lax.ppermute(lax.slice_in_dim(block, 0, width, axis=dim), axis, backward)
        block = jnp.concatenate([low, block, high], axis=dim)
    return block


def hines_solve(rhs, inverses, parents):
    number = inverses.shape[0]
    width = inverses.shape[1]
    blocks = rhs.reshape(number, width, rhs.shape[1])
    solved = []
    for segment in range(number):
        right = blocks[segment]
        if segment > 0:
            above = jnp.zeros_like(right)
            for earlier in range(segment):
                above = above + jnp.where(
                    parents[segment - 1] == earlier, solved[earlier], jnp.zeros_like(right)
                )
            right = right + coupling * above
        solved.append(
            jnp.dot(
                inverses[segment],
                right,
                precision=lax.Precision.HIGHEST,
                preferred_element_type=jnp.float32,
            )
        )
    return jnp.concatenate(solved, axis=0)


def neighbours(field):
    padded = jnp.pad(field, 1)
    beside = padded[2:, 1:-1, 1:-1] + padded[:-2, 1:-1, 1:-1]
    beside = beside + padded[1:-1, 2:, 1:-1] + padded[1:-1, :-2, 1:-1]
    return beside + padded[1:-1, 1:-1, 2:] + padded[1:-1, 1:-1, :-2]


def send_places(table):
    arrived = lax.all_to_all(table, ("slab", "row"), split_axis=0, concat_axis=0, tiled=True)
    return arrived


def send_currents(table):
    arrived = lax.all_to_all(table, ("slab", "row"), split_axis=0, concat_axis=0, tiled=True)
    return arrived


def send_potentials(table):
    arrived = lax.all_to_all(table, ("slab", "row"), split_axis=0, concat_axis=0, tiled=True)
    return arrived


def relax_grid(potential, source):
    depth_z = potential.shape[0]
    depth_y = potential.shape[1]
    stacked = jnp.stack([potential, source])
    extended = padded_2(stacked, (("slab", 1), ("row", 2)), SWEEPS)
    zplace = (
        lax.axis_index("slab") * depth_z
        - SWEEPS
        + jnp.arange(depth_z + 2 * SWEEPS, dtype=jnp.int32)
    )
    yplace = (
        lax.axis_index("row") * depth_y - SWEEPS + jnp.arange(depth_y + 2 * SWEEPS, dtype=jnp.int32)
    )
    zinside = (zplace >= 0) & (zplace < depth_z * lax.axis_size("slab"))
    yinside = (yplace >= 0) & (yplace < depth_y * lax.axis_size("row"))
    inside = zinside[:, None, None] & yinside[None, :, None]
    field = extended[0]
    feeding = extended[1]
    for repeat in range(SWEEPS):
        field = jnp.where(
            inside, (neighbours(field) + feeding) / (6.0 + screening), jnp.zeros_like(field)
        )
    result = field[SWEEPS:-SWEEPS, SWEEPS:-SWEEPS]
    return result


def shards(voltage, potential, transfer, conductance, inverses, parents, target, place):
    slabs = lax.axis_size("slab")
    lines = lax.axis_size("row")
    devices = slabs * lines
    local_cells = voltage.shape[1]
    capacity = max(2, 2 * local_cells // devices)
    patch_len = transfer.shape[0]
    positions = potential.size // patch_len
    owners = target[:, 0]
    one_hot = (owners[:, None] == jnp.arange(devices, dtype=jnp.int32)[None, :]).astype(jnp.int32)
    before = jnp.cumsum(one_hot, axis=0) - one_hot
    order_in = jnp.sum(before * one_hot, axis=1)
    slot_index = owners * capacity + order_in
    places = jnp.full((devices * capacity,), -1, jnp.int32).at[slot_index].set(place)
    arrived_places = send_places(places.reshape(devices, capacity)).reshape(devices * capacity)
    filled = arrived_places >= 0
    fetch_rows = jnp.where(filled, arrived_places, jnp.zeros_like(arrived_places))
    drop_rows = jnp.where(filled, arrived_places, jnp.full_like(arrived_places, positions))
    for timestep in range(STEPS):
        grid_rows = potential.reshape(positions, patch_len)
        picked = jnp.where(
            filled[:, None], grid_rows[fetch_rows], jnp.zeros((1, patch_len), jnp.float32)
        )
        returned = send_potentials(picked.reshape(devices, capacity, patch_len))
        sampled = returned.reshape(devices * capacity, patch_len)[slot_index]
        outside = lax.dot_general(
            transfer,
            sampled,
            (((0,), (1,)), ((), ())),
            precision=lax.Precision.HIGHEST,
            preferred_element_type=jnp.float32,
        )
        voltage = hines_solve(voltage + outside, inverses, parents)
        membrane = conductance[:, None] * (voltage - outside)
        deposit = jnp.dot(
            transfer, membrane, precision=lax.Precision.HIGHEST, preferred_element_type=jnp.float32
        )
        outgoing = (
            jnp.zeros((devices * capacity, patch_len), jnp.float32).at[slot_index].set(deposit.T)
        )
        arrived = send_currents(outgoing.reshape(devices, capacity, patch_len))
        summed = (
            jnp.zeros((positions, patch_len), jnp.float32)
            .at[drop_rows]
            .add(arrived.reshape(devices * capacity, patch_len), mode="drop")
        )
        source = summed.reshape(potential.shape)
        potential = relax_grid(potential, source)
    return (voltage, potential)


def solution(mesh):
    return jax.shard_map(
        shards,
        mesh=mesh,
        in_specs=(
            P(None, ("slab", "row")),
            P("slab", "row", None),
            P(),
            P(),
            P(),
            P(),
            P(("slab", "row"), None),
            P(("slab", "row")),
        ),
        out_specs=(P(None, ("slab", "row")), P("slab", "row", None)),
        check_vma=False,
    )
```

profile of v0, /device:TPU:34, one launch (start us, length us, event | category | flops | bytes accessed | tf_op | source)
XLA Modules:
  0.0 282.9 jit_solution(598044756614502851)
XLA Ops:
  2.3 3.5 %scatter_custom_fusion = s32[1536]{0:T(1024)S(1)} fusion(s32[768]{0:T(1024)S(1)} %fusion.315, s32[768]{0:T(1024)} %param.15, s32[]{:T(128)} %constant.75.clone.1), kind=kCustom, calls=%fused_computation.460 | custom fusion | bytes 6656 | tf_op jit(solution)/shard_map/scatter | solution.py:113
  6.6 10.2 %all-to-all-start = ((s32[128,1,12]{2,1,0:T(1,128)}), s32[128,1,12]{2,1,0:T(1,128)S(1)}, u32[]{:S(2)}, u32[]{:S(2)}) async-start(s32[128,1,12]{2,1,0:T(1,128)} %bitcast.3), calls=%async_computation | async-start | bytes 131072 | tf_op jit(solution)/shard_map/all_to_all | solution.py:60
  16.9 7.7 %all-to-all-done = s32[128,1,12]{2,1,0:T(1,128)S(1)} async-done(((s32[128,1,12]{2,1,0:T(1,128)}), s32[128,1,12]{2,1,0:T(1,128)S(1)}, u32[]{:S(2)}, u32[]{:S(2)}) %all-to-all-start) | async-done | bytes 6176 | tf_op jit(solution)/shard_map/all_to_all | solution.py:60
  26.1 2.6 gather_fusion
  30.3 6.7 %all-to-all-start.1 = ((f32[128,12,128]{2,1,0:T(8,128)}), f32[128,12,128]{2,1,0:T(8,128)S(1)}, u32[]{:S(2)}, u32[]{:S(2)}) async-start(f32[128,12,128]{2,1,0:T(8,128)} %broadcast_select_fusion.1), calls=%async_computation.1 | async-start | bytes 2097152 | tf_op jit(solution)/shard_map/all_to_all | solution.py:70
  56.9 2.9 %bitcast_add_fusion.1 = (f32[512,768]{1,0:T(8,128)S(1)}, f32[768,512]{0,1:T(8,128)S(1)}) fusion(f32[512,768]{1,0:T(8,128)} %param.8, f32[768,128]{1,0:T(8,128)S(1)} %gather_fusion.1, f32[128,512]{1,0:T(8,128)S(1)} %copy-done), kind=kOutput, calls=%fused_computation.124 | convolution fusion | flops 604372992 | bytes 5373952 | tf_op jit(solution)/shard_map/dot_general | solution.py:125
  64.0 2.7 fusion.56
  66.7 4.4 %scatter_custom_fusion.1 = f32[1536,128]{1,0:T(8,128)S(1)} fusion(s32[768]{0:T(1024)S(1)} %fusion.315, f32[768,128]{1,0:T(8,128)S(1)} %fusion.56, f32[]{:T(128)} %constant.80.clone.1), kind=kCustom, calls=%fused_computation.177 | custom fusion | bytes 786436 | tf_op jit(solution)/shard_map/scatter | solution.py:138
  71.2 27.2 %all_to_all.29 = f32[128,12,128]{2,1,0:T(8,128)S(1)} all-to-all(f32[128,12,128]{2,1,0:T(8,128)S(1)} %reshape.271), channel_id=1, replica_groups=mesh['slab'=32,'row'=4] {'slab','row'}, dimensions={0} | all-to-all | bytes 1572864 | tf_op jit(solution)/shard_map/all_to_all | solution.py:65
  98.5 9.2 %scatter_custom_fusion.2 = f32[2048,128]{1,0:T(8,128)S(1)} fusion(s32[1536]{0:T(1024)S(1)} %get-tuple-element.2, f32[1536,128]{1,0:T(8,128)S(1)} %reshape.329, f32[]{:T(128)} %constant.80.clone.1), kind=kCustom, calls=%fused_computation.165 | custom fusion | flops 196608 | bytes 1048580 | tf_op jit(solution)/shard_map/scatter-add | solution.py:144
  109.5 3.3 %collective-permute-start.1 = (f32[2,4,128,256]{3,2,1,0:T(8,128)}, f32[2,4,128,256]{3,2,1,0:T(8,128)S(1)}, u32[]{:S(2)}, u32[]{:S(2)}) collective-permute-start(f32[2,4,128,256]{3,2,1,0:T(8,128)} %get-tuple-element.23), channel_id=1, source_target_pairs={{4,0},{8,4},{12,8},{16,12},{20,16},{24,20},{28,24},{32,28},{36,32}... | collective-permute-start | bytes 3145736 | tf_op jit(solution)/shard_map/ppermute | solution.py:22
  114.8 10.6 %collective-permute-done.1 = f32[2,4,128,256]{3,2,1,0:T(8,128)S(1)} collective-permute-done((f32[2,4,128,256]{3,2,1,0:T(8,128)}, f32[2,4,128,256]{3,2,1,0:T(8,128)S(1)}, u32[]{:S(2)}, u32[]{:S(2)}) %collective-permute-start.1) | collective-permute-done | bytes 1048608 | tf_op jit(solution)/shard_map/ppermute | solution.py:22
  125.4 5.9 %collective-permute-done = f32[2,4,128,256]{3,2,1,0:T(8,128)} collective-permute-done((f32[2,4,128,256]{3,2,1,0:T(8,128)}, f32[2,4,128,256]{3,2,1,0:T(8,128)}, u32[]{:S(2)}, u32[]{:S(2)}) %collective-permute-start) | collective-permute-done | bytes 1048608 | tf_op jit(solution)/shard_map/ppermute | solution.py:19
  132.3 3.4 %collective-permute-start.3 = (f32[2,16,4,256]{3,2,1,0:T(4,128)S(1)}, f32[2,16,4,256]{3,2,1,0:T(4,128)S(1)}, u32[]{:S(2)}, u32[]{:S(2)}) collective-permute-start(f32[2,16,4,256]{3,2,1,0:T(4,128)S(1)} %get-tuple-element.11), channel_id=1, source_target_pairs={{1,0},{2,1},{3,2},{5,4},{6,5},{7,6},{9,8},{10,9},{11,10},{13,12},{... | collective-permute-start | bytes 393224 | tf_op jit(solution)/shard_map/ppermute | solution.py:22
  135.6 2.5 collective-permute-start.2
  139.1 3.4 %collective-permute-done.2 = f32[2,16,4,256]{3,2,1,0:T(4,128)S(1)} collective-permute-done((f32[2,16,4,256]{3,2,1,0:T(4,128)S(1)}, f32[2,16,4,256]{3,2,1,0:T(4,128)S(1)}, u32[]{:S(2)}, u32[]{:S(2)}) %collective-permute-start.2) | collective-permute-done | bytes 131104 | tf_op jit(solution)/shard_map/ppermute | solution.py:19
  152.0 4.3 %fusion.25 = (f32[16,136,256]{2,1,0:T(8,128)}, f32[16,136,256]{2,1,0:T(8,128)}, f32[16,136,256]{2,1,0:T(8,128)}, f32[16,136,256]{2,1,0:T(8,128)}) fusion(f32[16,136,256]{2,1,0:T(8,128)S(1)} %fusion.23), kind=kLoop, calls=%fused_computation.84 | loop fusion | flops 1114112 | bytes 11141120 | tf_op jit(solution)/shard_map/add | solution.py:55
  156.3 3.2 %fusion.65 = f32[8,128,256]{2,1,0:T(8,128)S(1)} fusion(f32[16,136,256]{2,1,0:T(8,128)} %get-tuple-element.7, f32[16,136,256]{2,1,0:T(8,128)} %get-tuple-element.19, f32[16,136,256]{2,1,0:T(8,128)} %get-tuple-element.18, f32[16,136,256]{2,1,0:T(8,128)} %get-tuple-element.17, f32[16,136,256]{2,1,0:T(8,128)} %get-tuple-element.16, pred[8,128]{1,0:T(8,128)(4,1)S(1)} %slice.479), kind=kLoop, calls=%fused_computation.156 | loop fusion | flops 1572864 | bytes 6292480 | tf_op jit(solution)/shard_map/jit(_where)/select_n | solution.py:93
  159.7 2.6 gather_fusion.2
  162.7 22.4 %all_to_all.30 = f32[128,12,128]{2,1,0:T(8,128)S(1)} all-to-all(f32[128,12,128]{2,1,0:T(8,128)S(1)} %broadcast_select_fusion), channel_id=1, replica_groups=mesh['slab'=32,'row'=4] {'slab','row'}, dimensions={0} | all-to-all | bytes 1572864 | tf_op jit(solution)/shard_map/all_to_all | solution.py:70
  186.8 2.9 %bitcast_add_fusion = (f32[512,768]{1,0:T(8,128)S(1)}, f32[768,512]{0,1:T(8,128)S(1)}) fusion(f32[512,768]{1,0:T(8,128)} %copy-done.2, f32[768,128]{1,0:T(8,128)S(1)} %gather_fusion.3, f32[128,512]{1,0:T(8,128)S(1)} %copy-done), kind=kOutput, calls=%fused_computation.120 | convolution fusion | flops 604372992 | bytes 5373952 | tf_op jit(solution)/shard_map/dot_general | solution.py:125
  193.9 2.7 fusion.53
  196.6 4.4 %scatter_custom_fusion.3 = f32[1536,128]{1,0:T(8,128)S(1)} fusion(s32[768]{0:T(1024)S(1)} %fusion.315, f32[768,128]{1,0:T(8,128)S(1)} %fusion.53, f32[]{:T(128)} %constant.80.clone.1), kind=kCustom, calls=%fused_computation.175 | custom fusion | bytes 786436 | tf_op jit(solution)/shard_map/scatter | solution.py:138
  201.0 23.0 %all_to_all.31 = f32[128,12,128]{2,1,0:T(8,128)S(1)} all-to-all(f32[128,12,128]{2,1,0:T(8,128)S(1)} %reshape.275), channel_id=1, replica_groups=mesh['slab'=32,'row'=4] {'slab','row'}, dimensions={0} | all-to-all | bytes 1572864 | tf_op jit(solution)/shard_map/all_to_all | solution.py:65
  224.1 9.0 %scatter_custom_fusion.4 = f32[2048,128]{1,0:T(8,128)S(1)} fusion(s32[1536]{0:T(1024)S(1)} %get-tuple-element.2, f32[1536,128]{1,0:T(8,128)S(1)} %reshape.345, f32[]{:T(128)} %constant.80.clone.1), kind=kCustom, calls=%fused_computation.163 | custom fusion | flops 196608 | bytes 1048580 | tf_op jit(solution)/shard_map/scatter-add | solution.py:144
  233.6 3.6 %collective-permute-start.5 = (f32[2,4,128,256]{3,2,1,0:T(8,128)S(1)}, f32[2,4,128,256]{3,2,1,0:T(8,128)S(1)}, u32[]{:S(2)}, u32[]{:S(2)}) collective-permute-start(f32[2,4,128,256]{3,2,1,0:T(8,128)S(1)} %get-tuple-element.21), channel_id=1, source_target_pairs={{4,0},{8,4},{12,8},{16,12},{20,16},{24,20},{28,24},{32,28},{36,32}... | collective-permute-start | bytes 3145736 | tf_op jit(solution)/shard_map/ppermute | solution.py:22
  239.1 10.4 %collective-permute-done.5 = f32[2,4,128,256]{3,2,1,0:T(8,128)S(1)} collective-permute-done((f32[2,4,128,256]{3,2,1,0:T(8,128)S(1)}, f32[2,4,128,256]{3,2,1,0:T(8,128)S(1)}, u32[]{:S(2)}, u32[]{:S(2)}) %collective-permute-start.5) | collective-permute-done | bytes 1048608 | tf_op jit(solution)/shard_map/ppermute | solution.py:22
  249.4 5.9 %collective-permute-done.4 = f32[2,4,128,256]{3,2,1,0:T(8,128)S(1)} collective-permute-done((f32[2,4,128,256]{3,2,1,0:T(8,128)S(1)}, f32[2,4,128,256]{3,2,1,0:T(8,128)S(1)}, u32[]{:S(2)}, u32[]{:S(2)}) %collective-permute-start.4) | collective-permute-done | bytes 1048608 | tf_op jit(solution)/shard_map/ppermute | solution.py:19
  255.4 3.4 %collective-permute-start.7 = (f32[2,16,4,256]{3,2,1,0:T(4,128)S(1)}, f32[2,16,4,256]{3,2,1,0:T(4,128)S(1)}, u32[]{:S(2)}, u32[]{:S(2)}) collective-permute-start(f32[2,16,4,256]{3,2,1,0:T(4,128)S(1)} %get-tuple-element.9), channel_id=1, source_target_pairs={{1,0},{2,1},{3,2},{5,4},{6,5},{7,6},{9,8},{10,9},{11,10},{13,12},{... | collective-permute-start | bytes 393224 | tf_op jit(solution)/shard_map/ppermute | solution.py:22
  262.3 3.4 %collective-permute-done.6 = f32[2,16,4,256]{3,2,1,0:T(4,128)S(1)} collective-permute-done((f32[2,16,4,256]{3,2,1,0:T(4,128)S(1)}, f32[2,16,4,256]{3,2,1,0:T(4,128)S(1)}, u32[]{:S(2)}, u32[]{:S(2)}) %collective-permute-start.6) | collective-permute-done | bytes 131104 | tf_op jit(solution)/shard_map/ppermute | solution.py:19
  274.1 4.3 %fusion.51 = (f32[16,136,256]{2,1,0:T(8,128)}, f32[16,136,256]{2,1,0:T(8,128)}, f32[16,136,256]{2,1,0:T(8,128)}, f32[16,136,256]{2,1,0:T(8,128)}) fusion(f32[16,136,256]{2,1,0:T(8,128)S(1)} %fusion.49), kind=kLoop, calls=%fused_computation.110 | loop fusion | flops 1114112 | bytes 11141120 | tf_op jit(solution)/shard_map/add | solution.py:55
  278.4 4.2 %fusion.63 = f32[8,128,256]{2,1,0:T(8,128)} fusion(f32[16,136,256]{2,1,0:T(8,128)} %get-tuple-element.5, f32[16,136,256]{2,1,0:T(8,128)} %get-tuple-element.15, f32[16,136,256]{2,1,0:T(8,128)} %get-tuple-element.14, f32[16,136,256]{2,1,0:T(8,128)} %get-tuple-element.13, f32[16,136,256]{2,1,0:T(8,128)} %get-tuple-element.12, pred[8,128]{1,0:T(8,128)(4,1)S(1)} %slice.479), kind=kLoop, calls=%fused_computation.149 | loop fusion | flops 1572864 | bytes 6292480 | tf_op jit(solution)/shard_map/jit(_where)/select_n | solution.py:93
  (94 shorter events, 47.9 us)
Async XLA Ops:
  0.6 56.2 %copy-start = (f32[128,512]{1,0:T(8,128)S(1)}, f32[128,512]{1,0:T(8,128)}, u32[]{:S(2)}) copy-start(f32[128,512]{1,0:T(8,128)} %param.10) | copy-start | bytes 786436
  0.6 1.6 copy-start.7
  0.7 16.1 %copy-start.1 = (f32[8,128,256]{2,1,0:T(8,128)S(1)}, f32[8,128,256]{2,1,0:T(8,128)}, u32[]{:S(2)}) copy-start(f32[8,128,256]{2,1,0:T(8,128)} %param.9) | copy-start | bytes 3145732
  6.6 18.0 %all-to-all-start = ((s32[128,1,12]{2,1,0:T(1,128)}), s32[128,1,12]{2,1,0:T(1,128)S(1)}, u32[]{:S(2)}, u32[]{:S(2)}) async-start(s32[128,1,12]{2,1,0:T(1,128)} %bitcast.3), calls=%async_computation | async-start | bytes 131072 | tf_op jit(solution)/shard_map/all_to_all | solution.py:60
  28.8 8.3 %copy-start.6 = (s32[7]{0:T(128)S(1)}, s32[7]{0:T(128)}, u32[]{:S(2)}) copy-start(s32[7]{0:T(128)} %param.13) | copy-start | bytes 88
  30.3 24.9 %all-to-all-start.1 = ((f32[128,12,128]{2,1,0:T(8,128)}), f32[128,12,128]{2,1,0:T(8,128)S(1)}, u32[]{:S(2)}, u32[]{:S(2)}) async-start(f32[128,12,128]{2,1,0:T(8,128)} %broadcast_select_fusion.1), calls=%async_computation.1 | async-start | bytes 2097152 | tf_op jit(solution)/shard_map/all_to_all | solution.py:70
  56.9 2.9 %copy-start.4 = (f32[8,64,64]{2,1,0:T(8,128)S(1)}, f32[8,64,64]{2,1,0:T(8,128)}, u32[]{:S(2)}) copy-start(f32[8,64,64]{2,1,0:T(8,128)} %param.12) | copy-start | bytes 393220
  61.6 2.4 copy-start.8
  62.9 1.1 copy-start.2
  109.5 15.9 %collective-permute-start.1 = (f32[2,4,128,256]{3,2,1,0:T(8,128)}, f32[2,4,128,256]{3,2,1,0:T(8,128)S(1)}, u32[]{:S(2)}, u32[]{:S(2)}) collective-permute-start(f32[2,4,128,256]{3,2,1,0:T(8,128)} %get-tuple-element.23), channel_id=1, source_target_pairs={{4,0},{8,4},{12,8},{16,12},{20,16},{24,20},{28,24},{32,28},{36,32}... | collective-permute-start | bytes 3145736 | tf_op jit(solution)/shard_map/ppermute | solution.py:22
  112.8 18.5 %collective-permute-start = (f32[2,4,128,256]{3,2,1,0:T(8,128)}, f32[2,4,128,256]{3,2,1,0:T(8,128)}, u32[]{:S(2)}, u32[]{:S(2)}) collective-permute-start(f32[2,4,128,256]{3,2,1,0:T(8,128)} %get-tuple-element.22), channel_id=1, source_target_pairs={{0,4},{4,8},{8,12},{12,16},{16,20},{20,24},{24,28},{28,32},{32,36}... | collective-permute-start | bytes 3145736 | tf_op jit(solution)/shard_map/ppermute | solution.py:19
  132.3 6.9 %collective-permute-start.3 = (f32[2,16,4,256]{3,2,1,0:T(4,128)S(1)}, f32[2,16,4,256]{3,2,1,0:T(4,128)S(1)}, u32[]{:S(2)}, u32[]{:S(2)}) collective-permute-start(f32[2,16,4,256]{3,2,1,0:T(4,128)S(1)} %get-tuple-element.11), channel_id=1, source_target_pairs={{1,0},{2,1},{3,2},{5,4},{6,5},{7,6},{9,8},{10,9},{11,10},{13,12},{... | collective-permute-start | bytes 393224 | tf_op jit(solution)/shard_map/ppermute | solution.py:22
  135.6 6.9 %collective-permute-start.2 = (f32[2,16,4,256]{3,2,1,0:T(4,128)S(1)}, f32[2,16,4,256]{3,2,1,0:T(4,128)S(1)}, u32[]{:S(2)}, u32[]{:S(2)}) collective-permute-start(f32[2,16,4,256]{3,2,1,0:T(4,128)S(1)} %get-tuple-element.10), channel_id=1, source_target_pairs={{0,1},{1,2},{2,3},{4,5},{5,6},{6,7},{8,9},{9,10},{10,11},{12,13},{... | collective-permute-start | bytes 393224 | tf_op jit(solution)/shard_map/ppermute | solution.py:19
  186.8 2.9 %copy-start.5 = (f32[8,64,64]{2,1,0:T(8,128)S(1)}, f32[8,64,64]{2,1,0:T(8,128)}, u32[]{:S(2)}) copy-start(f32[8,64,64]{2,1,0:T(8,128)} %param.12) | copy-start | bytes 393220
  192.7 1.1 copy-start.3
  233.6 15.9 %collective-permute-start.5 = (f32[2,4,128,256]{3,2,1,0:T(8,128)S(1)}, f32[2,4,128,256]{3,2,1,0:T(8,128)S(1)}, u32[]{:S(2)}, u32[]{:S(2)}) collective-permute-start(f32[2,4,128,256]{3,2,1,0:T(8,128)S(1)} %get-tuple-element.21), channel_id=1, source_target_pairs={{4,0},{8,4},{12,8},{16,12},{20,16},{24,20},{28,24},{32,28},{36,32}... | collective-permute-start | bytes 3145736 | tf_op jit(solution)/shard_map/ppermute | solution.py:22
  237.1 18.2 %collective-permute-start.4 = (f32[2,4,128,256]{3,2,1,0:T(8,128)S(1)}, f32[2,4,128,256]{3,2,1,0:T(8,128)S(1)}, u32[]{:S(2)}, u32[]{:S(2)}) collective-permute-start(f32[2,4,128,256]{3,2,1,0:T(8,128)S(1)} %get-tuple-element.20), channel_id=1, source_target_pairs={{0,4},{4,8},{8,12},{12,16},{16,20},{20,24},{24,28},{28,32},{32,36}... | collective-permute-start | bytes 3145736 | tf_op jit(solution)/shard_map/ppermute | solution.py:19
  255.4 6.9 %collective-permute-start.7 = (f32[2,16,4,256]{3,2,1,0:T(4,128)S(1)}, f32[2,16,4,256]{3,2,1,0:T(4,128)S(1)}, u32[]{:S(2)}, u32[]{:S(2)}) collective-permute-start(f32[2,16,4,256]{3,2,1,0:T(4,128)S(1)} %get-tuple-element.9), channel_id=1, source_target_pairs={{1,0},{2,1},{3,2},{5,4},{6,5},{7,6},{9,8},{10,9},{11,10},{13,12},{... | collective-permute-start | bytes 393224 | tf_op jit(solution)/shard_map/ppermute | solution.py:22
  258.8 6.9 %collective-permute-start.6 = (f32[2,16,4,256]{3,2,1,0:T(4,128)S(1)}, f32[2,16,4,256]{3,2,1,0:T(4,128)S(1)}, u32[]{:S(2)}, u32[]{:S(2)}) collective-permute-start(f32[2,16,4,256]{3,2,1,0:T(4,128)S(1)} %get-tuple-element.8), channel_id=1, source_target_pairs={{0,1},{1,2},{2,3},{4,5},{5,6},{6,7},{8,9},{9,10},{10,11},{12,13},{... | collective-permute-start | bytes 393224 | tf_op jit(solution)/shard_map/ppermute | solution.py:19
where the time goes:
time: 287 us; the launch traced here: 283 us
  blocking collectives  72.7 us (25%)
  other arithmetic  55.5 us (19%)
  waiting for transfers between devices  49.2 us (17%)
  starting transfers between devices  39.4 us (14%)
  local copies, waits for them, and re-layouts  30 us (10%)
  between operations  19.1 us (7%)
  matrix products  17.2 us (6%)
    all_to_all x2, blocking collectives, send_currents(): lax.all_to_all(table, ('slab', 'row'), split_axis=0, concat_axis=0, tiled...  50.3 us
    ppermute x4, waiting for transfers between devices, padded_2(): lax.ppermute(lax.slice_in_dim(block, 0, width, axis=dim), axis, backward)  22.9 us
    all_to_all x1, blocking collectives, send_potentials(): lax.all_to_all(table, ('slab', 'row'), split_axis=0, concat_axis=0, tiled...  22.4 us
    select_n x8, other arithmetic, relax_grid(): jnp.where(inside, (neighbours(field) + feeding) / (6.0 + screening), jnp....  19.6 us
    ppermute x4, waiting for transfers between devices, padded_2(): lax.ppermute(lax.slice_in_dim(block, block.shape[dim] - width, None, axis...  18.6 us
    scatter-add x2, other arithmetic, shards(): summed = jnp.zeros((positions, patch_len), jnp.float32).at[drop_rows].add...  18.2 us
    ppermute x4, starting transfers between devices, padded_2(): lax.ppermute(lax.slice_in_dim(block, 0, width, axis=dim), axis, backward)  13.6 us
    all_to_all x1, starting transfers between devices, send_places(): lax.all_to_all(table, ('slab', 'row'), split_axis=0, concat_axis=0, tiled...  10.2 us
  transfers between devices with their start and end apart: 10, of which 9 were waited for; matrix products, arithmetic and copies ran while one was open for 0% of the time, Pallas kernels for 0%

commit v1 on v0

--- a/solution.py
+++ b/solution.py
@@ -1,6 +1,9 @@
-import jax
-import jax.numpy as jnp
+import functools
+import jax, jax.numpy as jnp
 from jax import lax
+from jax.experimental import pallas as pl
+from jax.experimental.pallas import tpu as pltpu
+
 from jax.sharding import PartitionSpec as P
 
 STEPS = 2
@@ -56,18 +59,54 @@
     return beside + padded[1:-1, 1:-1, 2:] + padded[1:-1, 1:-1, :-2]
 
 
+def peer_of(offset):
+    slab = lax.axis_index("slab"); row = lax.axis_index("row")
+    core = (slab + offset) % 2
+    y = (slab // 2 + offset // 2) % 4
+    x = (row + offset // 8) % 4
+    z = (slab // 8 + offset // 32) % 4
+    return z * 8 + y * 2 + core, x
+
+def kernel(table, out, send_sem, recv_sem):
+    slab = lax.axis_index("slab"); row = lax.axis_index("row")
+    me = slab * 4 + row
+    barrier = pltpu.get_barrier_semaphore()
+    def greet(o, c):
+        s, r = peer_of(o)
+        pl.semaphore_signal(barrier, inc=1, device_id={"slab": s, "row": r})
+        return c
+    lax.fori_loop(1, 128, greet, 0)
+    pl.semaphore_wait(barrier, 127)
+    def send(o, c):
+        s, r = peer_of(o)
+        pltpu.make_async_remote_copy(
+            src_ref=table.at[s * 4 + r], dst_ref=out.at[me], send_sem=send_sem, recv_sem=recv_sem,
+            device_id={"slab": s, "row": r}).start()
+        return c
+    lax.fori_loop(1, 128, send, 0)
+    out[me] = table[me]
+    pltpu.make_async_copy(table.at[pl.ds(0, 127)], out.at[pl.ds(0, 127)], recv_sem).wait()
+    pltpu.make_async_copy(table.at[pl.ds(0, 127)], table.at[pl.ds(0, 127)], send_sem).wait()
+
+def a2a(table, cid):
+    return pl.pallas_call(kernel, out_shape=jax.ShapeDtypeStruct(table.shape, table.dtype),
+        in_specs=[pl.BlockSpec(memory_space=pltpu.VMEM)], out_specs=pl.BlockSpec(memory_space=pltpu.VMEM),
+        scratch_shapes=[pltpu.SemaphoreType.DMA, pltpu.SemaphoreType.DMA],
+        compiler_params=pltpu.CompilerParams(collective_id=cid, has_side_effects=True))(table)
+
+
 def send_places(table):
     arrived = lax.all_to_all(table, ("slab", "row"), split_axis=0, concat_axis=0, tiled=True)
     return arrived
 
 
 def send_currents(table):
-    arrived = lax.all_to_all(table, ("slab", "row"), split_axis=0, concat_axis=0, tiled=True)
+    arrived = a2a(table, 0)
     return arrived
 
 
 def send_potentials(table):
-    arrived = lax.all_to_all(table, ("slab", "row"), split_axis=0, concat_axis=0, tiled=True)
+    arrived = a2a(table, 0)
     return arrived
 
 

time: 287 us -> 305 us (1.063)
  the two profiles are of different devices: /device:TPU:34 before, /device:TPU:36 now
where the time goes in v1:
time: 305 us; the launch traced here: 302 us
  Pallas kernels  99.2 us (33%)
  other arithmetic  56.4 us (18%)
  waiting for transfers between devices  40.9 us (13%)
  local copies, waits for them, and re-layouts  37.2 us (12%)
  starting transfers between devices  31.4 us (10%)
  between operations  19.2 us (6%)
  matrix products  17.2 us (6%)
    pallas_call x4, Pallas kernels, a2a(): pl.pallas_call(kernel, out_shape=jax.ShapeDtypeStruct(table.shape, table....  99.2 us
    ppermute x4, waiting for transfers between devices, padded_2(): lax.ppermute(lax.slice_in_dim(block, 0, width, axis=dim), axis, backward)  22 us
    select_n x8, other arithmetic, relax_grid(): jnp.where(inside, (neighbours(field) + feeding) / (6.0 + screening), jnp....  19.6 us
    ppermute x4, waiting for transfers between devices, padded_2(): lax.ppermute(lax.slice_in_dim(block, block.shape[dim] - width, None, axis...  18.8 us
    scatter-add x2, other arithmetic, shards(): summed = jnp.zeros((positions, patch_len), jnp.float32).at[drop_rows].add...  18 us
    ppermute x4, starting transfers between devices, padded_2(): lax.ppermute(lax.slice_in_dim(block, 0, width, axis=dim), axis, backward)  11.2 us
    all_to_all x1, starting transfers between devices, send_places(): lax.all_to_all(table, ('slab', 'row'), split_axis=0, concat_axis=0, tiled...  10.8 us
    ppermute x4, starting transfers between devices, padded_2(): lax.ppermute(lax.slice_in_dim(block, block.shape[dim] - width, None, axis...  9.38 us
  transfers between devices with their start and end apart: 9, of which 8 were waited for; matrix products, arithmetic and copies ran while one was open for 0% of the time, Pallas kernels for 0%

profile of v1, /device:TPU:36, one launch (start us, length us, event | category | flops | bytes accessed | tf_op | source)
XLA Modules:
  0.0 301.6 jit_solution(7868153889601637451)
XLA Ops:
  2.3 3.5 %scatter_custom_fusion = s32[1536]{0:T(1024)S(1)} fusion(s32[768]{0:T(1024)S(1)} %fusion.315, s32[768]{0:T(1024)} %param.15, s32[]{:T(128)} %constant.75.clone.1), kind=kCustom, calls=%fused_computation.460 | custom fusion | bytes 6656 | tf_op jit(solution)/shard_map/scatter | solution.py:152
  6.6 10.8 %all-to-all-start = ((s32[128,1,12]{2,1,0:T(1,128)}), s32[128,1,12]{2,1,0:T(1,128)S(1)}, u32[]{:S(2)}, u32[]{:S(2)}) async-start(s32[128,1,12]{2,1,0:T(1,128)} %bitcast.3), calls=%async_computation | async-start | bytes 131072 | tf_op jit(solution)/shard_map/all_to_all | solution.py:99
  37.3 2.6 gather_fusion
  41.5 25.4 %shard_map.95 = f32[128,12,128]{2,1,0:T(8,128)} custom-call(f32[128,12,128]{2,1,0:T(8,128)} %broadcast_select_fusion.1.table), custom_call_target="tpu_custom_call" | custom-call | tf_op jit(solution)/shard_map/pallas_call | solution.py:92
  69.8 2.9 bitcast_add_fusion.1
  76.9 2.7 fusion.56
  79.6 4.5 %scatter_custom_fusion.1 = f32[1536,128]{1,0:T(8,128)S(1)} fusion(s32[768]{0:T(1024)S(1)} %fusion.315, f32[768,128]{1,0:T(8,128)S(1)} %fusion.56, f32[]{:T(128)} %constant.80.clone.1), kind=kCustom, calls=%fused_computation.177 | custom fusion | bytes 786436 | tf_op jit(solution)/shard_map/scatter | solution.py:177
  85.2 24.6 %shard_map.96 = f32[128,12,128]{2,1,0:T(8,128)} custom-call(f32[128,12,128]{2,1,0:T(8,128)} %reshape.271.table), custom_call_target="tpu_custom_call" | custom-call | tf_op jit(solution)/shard_map/pallas_call | solution.py:92
  111.1 9.0 %scatter_custom_fusion.2 = f32[2048,128]{1,0:T(8,128)S(1)} fusion(s32[1536]{0:T(1024)S(1)} %get-tuple-element.2, f32[1536,128]{1,0:T(8,128)S(1)} %reshape.329, f32[]{:T(128)} %constant.80.clone.1), kind=kCustom, calls=%fused_computation.165 | custom fusion | flops 196608 | bytes 1048580 | tf_op jit(solution)/shard_map/scatter-add | solution.py:183
  124.0 2.2 collective-permute-start
  126.3 10.3 %collective-permute-done.1 = f32[2,4,128,256]{3,2,1,0:T(8,128)S(1)} collective-permute-done((f32[2,4,128,256]{3,2,1,0:T(8,128)}, f32[2,4,128,256]{3,2,1,0:T(8,128)S(1)}, u32[]{:S(2)}, u32[]{:S(2)}) %collective-permute-start.1) | collective-permute-done | bytes 1048608 | tf_op jit(solution)/shard_map/ppermute | solution.py:25
  136.6 5.9 %collective-permute-done = f32[2,4,128,256]{3,2,1,0:T(8,128)} collective-permute-done((f32[2,4,128,256]{3,2,1,0:T(8,128)}, f32[2,4,128,256]{3,2,1,0:T(8,128)}, u32[]{:S(2)}, u32[]{:S(2)}) %collective-permute-start) | collective-permute-done | bytes 1048608 | tf_op jit(solution)/shard_map/ppermute | solution.py:22
  143.5 2.8 collective-permute-start.3
  146.3 3.0 %collective-permute-start.2 = (f32[2,16,4,256]{3,2,1,0:T(4,128)S(1)}, f32[2,16,4,256]{3,2,1,0:T(4,128)S(1)}, u32[]{:S(2)}, u32[]{:S(2)}) collective-permute-start(f32[2,16,4,256]{3,2,1,0:T(4,128)S(1)} %get-tuple-element.10), channel_id=1, source_target_pairs={{0,1},{1,2},{2,3},{4,5},{5,6},{6,7},{8,9},{9,10},{10,11},{12,13},{... | collective-permute-start | bytes 393224 | tf_op jit(solution)/shard_map/ppermute | solution.py:22
  150.3 2.8 collective-permute-done.2
  162.7 4.3 %fusion.25 = (f32[16,136,256]{2,1,0:T(8,128)}, f32[16,136,256]{2,1,0:T(8,128)}, f32[16,136,256]{2,1,0:T(8,128)}, f32[16,136,256]{2,1,0:T(8,128)}) fusion(f32[16,136,256]{2,1,0:T(8,128)S(1)} %fusion.23), kind=kLoop, calls=%fused_computation.84 | loop fusion | flops 1114112 | bytes 11141120 | tf_op jit(solution)/shard_map/add | solution.py:58
  166.9 3.2 %fusion.65 = f32[8,128,256]{2,1,0:T(8,128)S(1)} fusion(f32[16,136,256]{2,1,0:T(8,128)} %get-tuple-element.7, f32[16,136,256]{2,1,0:T(8,128)} %get-tuple-element.19, f32[16,136,256]{2,1,0:T(8,128)} %get-tuple-element.18, f32[16,136,256]{2,1,0:T(8,128)} %get-tuple-element.17, f32[16,136,256]{2,1,0:T(8,128)} %get-tuple-element.16, pred[8,128]{1,0:T(8,128)(4,1)S(1)} %slice.479), kind=kLoop, calls=%fused_computation.156 | loop fusion | flops 1572864 | bytes 6292480 | tf_op jit(solution)/shard_map/jit(_where)/select_n | solution.py:132
  170.3 2.6 gather_fusion.2
  174.3 23.5 %shard_map.97 = f32[128,12,128]{2,1,0:T(8,128)} custom-call(f32[128,12,128]{2,1,0:T(8,128)} %broadcast_select_fusion.table), custom_call_target="tpu_custom_call" | custom-call | tf_op jit(solution)/shard_map/pallas_call | solution.py:92
  200.9 2.9 bitcast_add_fusion
  208.0 2.7 fusion.53
  210.7 4.4 %scatter_custom_fusion.3 = f32[1536,128]{1,0:T(8,128)S(1)} fusion(s32[768]{0:T(1024)S(1)} %fusion.315, f32[768,128]{1,0:T(8,128)S(1)} %fusion.53, f32[]{:T(128)} %constant.80.clone.1), kind=kCustom, calls=%fused_computation.175 | custom fusion | bytes 786436 | tf_op jit(solution)/shard_map/scatter | solution.py:177
  216.1 25.8 %shard_map.98 = f32[128,12,128]{2,1,0:T(8,128)} custom-call(f32[128,12,128]{2,1,0:T(8,128)} %reshape.275.table), custom_call_target="tpu_custom_call" | custom-call | tf_op jit(solution)/shard_map/pallas_call | solution.py:92
  243.2 9.0 %scatter_custom_fusion.4 = f32[2048,128]{1,0:T(8,128)S(1)} fusion(s32[1536]{0:T(1024)S(1)} %get-tuple-element.2, f32[1536,128]{1,0:T(8,128)S(1)} %reshape.345, f32[]{:T(128)} %constant.80.clone.1), kind=kCustom, calls=%fused_computation.163 | custom fusion | flops 196608 | bytes 1048580 | tf_op jit(solution)/shard_map/scatter-add | solution.py:183
  252.6 2.2 collective-permute-start.5
  254.8 2.2 collective-permute-start.4
  257.0 10.1 %collective-permute-done.5 = f32[2,4,128,256]{3,2,1,0:T(8,128)S(1)} collective-permute-done((f32[2,4,128,256]{3,2,1,0:T(8,128)S(1)}, f32[2,4,128,256]{3,2,1,0:T(8,128)S(1)}, u32[]{:S(2)}, u32[]{:S(2)}) %collective-permute-start.5) | collective-permute-done | bytes 1048608 | tf_op jit(solution)/shard_map/ppermute | solution.py:25
  267.1 5.9 %collective-permute-done.4 = f32[2,4,128,256]{3,2,1,0:T(8,128)S(1)} collective-permute-done((f32[2,4,128,256]{3,2,1,0:T(8,128)S(1)}, f32[2,4,128,256]{3,2,1,0:T(8,128)S(1)}, u32[]{:S(2)}, u32[]{:S(2)}) %collective-permute-start.4) | collective-permute-done | bytes 1048608 | tf_op jit(solution)/shard_map/ppermute | solution.py:22
  273.1 4.2 %collective-permute-start.7 = (f32[2,16,4,256]{3,2,1,0:T(4,128)S(1)}, f32[2,16,4,256]{3,2,1,0:T(4,128)S(1)}, u32[]{:S(2)}, u32[]{:S(2)}) collective-permute-start(f32[2,16,4,256]{3,2,1,0:T(4,128)S(1)} %get-tuple-element.9), channel_id=1, source_target_pairs={{1,0},{2,1},{3,2},{5,4},{6,5},{7,6},{9,8},{10,9},{11,10},{13,12},{... | collective-permute-start | bytes 393224 | tf_op jit(solution)/shard_map/ppermute | solution.py:25
  279.9 4.2 %collective-permute-done.6 = f32[2,16,4,256]{3,2,1,0:T(4,128)S(1)} collective-permute-done((f32[2,16,4,256]{3,2,1,0:T(4,128)S(1)}, f32[2,16,4,256]{3,2,1,0:T(4,128)S(1)}, u32[]{:S(2)}, u32[]{:S(2)}) %collective-permute-start.6) | collective-permute-done | bytes 131104 | tf_op jit(solution)/shard_map/ppermute | solution.py:22
  292.8 4.3 %fusion.51 = (f32[16,136,256]{2,1,0:T(8,128)}, f32[16,136,256]{2,1,0:T(8,128)}, f32[16,136,256]{2,1,0:T(8,128)}, f32[16,136,256]{2,1,0:T(8,128)}) fusion(f32[16,136,256]{2,1,0:T(8,128)S(1)} %fusion.49), kind=kLoop, calls=%fused_computation.110 | loop fusion | flops 1114112 | bytes 11141120 | tf_op jit(solution)/shard_map/add | solution.py:58
  297.1 4.2 %fusion.63 = f32[8,128,256]{2,1,0:T(8,128)} fusion(f32[16,136,256]{2,1,0:T(8,128)} %get-tuple-element.5, f32[16,136,256]{2,1,0:T(8,128)} %get-tuple-element.15, f32[16,136,256]{2,1,0:T(8,128)} %get-tuple-element.14, f32[16,136,256]{2,1,0:T(8,128)} %get-tuple-element.13, f32[16,136,256]{2,1,0:T(8,128)} %get-tuple-element.12, pred[8,128]{1,0:T(8,128)(4,1)S(1)} %slice.479), kind=kLoop, calls=%fused_computation.149 | loop fusion | flops 1572864 | bytes 6292480 | tf_op jit(solution)/shard_map/jit(_where)/select_n | solution.py:132
  (93 shorter events, 53.6 us)
Async XLA Ops:
  0.6 69.1 %copy-start = (f32[128,512]{1,0:T(8,128)S(1)}, f32[128,512]{1,0:T(8,128)}, u32[]{:S(2)}) copy-start(f32[128,512]{1,0:T(8,128)} %param.10) | copy-start | bytes 786436
  0.6 1.6 copy-start.7
  0.7 16.8 %copy-start.6 = (s32[7]{0:T(128)S(1)}, s32[7]{0:T(128)}, u32[]{:S(2)}) copy-start(s32[7]{0:T(128)} %param.13) | copy-start | bytes 88
  0.7 33.7 %copy-start.1 = (f32[8,128,256]{2,1,0:T(8,128)S(1)}, f32[8,128,256]{2,1,0:T(8,128)}, u32[]{:S(2)}) copy-start(f32[8,128,256]{2,1,0:T(8,128)} %param.9) | copy-start | bytes 3145732
  6.6 29.2 %all-to-all-start = ((s32[128,1,12]{2,1,0:T(1,128)}), s32[128,1,12]{2,1,0:T(1,128)S(1)}, u32[]{:S(2)}, u32[]{:S(2)}) async-start(s32[128,1,12]{2,1,0:T(1,128)} %bitcast.3), calls=%async_computation | async-start | bytes 131072 | tf_op jit(solution)/shard_map/all_to_all | solution.py:99
  69.7 2.9 copy-start.4
  74.5 2.4 copy-start.8
  75.7 1.1 copy-start.2
  121.9 14.7 %collective-permute-start.1 = (f32[2,4,128,256]{3,2,1,0:T(8,128)}, f32[2,4,128,256]{3,2,1,0:T(8,128)S(1)}, u32[]{:S(2)}, u32[]{:S(2)}) collective-permute-start(f32[2,4,128,256]{3,2,1,0:T(8,128)} %get-tuple-element.23), channel_id=1, source_target_pairs={{4,0},{8,4},{12,8},{16,12},{20,16},{24,20},{28,24},{32,28},{36,32}... | collective-permute-start | bytes 3145736 | tf_op jit(solution)/shard_map/ppermute | solution.py:25
  124.0 18.5 %collective-permute-start = (f32[2,4,128,256]{3,2,1,0:T(8,128)}, f32[2,4,128,256]{3,2,1,0:T(8,128)}, u32[]{:S(2)}, u32[]{:S(2)}) collective-permute-start(f32[2,4,128,256]{3,2,1,0:T(8,128)} %get-tuple-element.22), channel_id=1, source_target_pairs={{0,4},{4,8},{8,12},{12,16},{16,20},{20,24},{24,28},{28,32},{32,36}... | collective-permute-start | bytes 3145736 | tf_op jit(solution)/shard_map/ppermute | solution.py:22
  143.5 6.9 %collective-permute-start.3 = (f32[2,16,4,256]{3,2,1,0:T(4,128)S(1)}, f32[2,16,4,256]{3,2,1,0:T(4,128)S(1)}, u32[]{:S(2)}, u32[]{:S(2)}) collective-permute-start(f32[2,16,4,256]{3,2,1,0:T(4,128)S(1)} %get-tuple-element.11), channel_id=1, source_target_pairs={{1,0},{2,1},{3,2},{5,4},{6,5},{7,6},{9,8},{10,9},{11,10},{13,12},{... | collective-permute-start | bytes 393224 | tf_op jit(solution)/shard_map/ppermute | solution.py:25
  146.3 6.9 %collective-permute-start.2 = (f32[2,16,4,256]{3,2,1,0:T(4,128)S(1)}, f32[2,16,4,256]{3,2,1,0:T(4,128)S(1)}, u32[]{:S(2)}, u32[]{:S(2)}) collective-permute-start(f32[2,16,4,256]{3,2,1,0:T(4,128)S(1)} %get-tuple-element.10), channel_id=1, source_target_pairs={{0,1},{1,2},{2,3},{4,5},{5,6},{6,7},{8,9},{9,10},{10,11},{12,13},{... | collective-permute-start | bytes 393224 | tf_op jit(solution)/shard_map/ppermute | solution.py:22
  200.8 2.9 copy-start.5
  206.8 1.1 copy-start.3
  252.6 14.5 %collective-permute-start.5 = (f32[2,4,128,256]{3,2,1,0:T(8,128)S(1)}, f32[2,4,128,256]{3,2,1,0:T(8,128)S(1)}, u32[]{:S(2)}, u32[]{:S(2)}) collective-permute-start(f32[2,4,128,256]{3,2,1,0:T(8,128)S(1)} %get-tuple-element.21), channel_id=1, source_target_pairs={{4,0},{8,4},{12,8},{16,12},{20,16},{24,20},{28,24},{32,28},{36,32}... | collective-permute-start | bytes 3145736 | tf_op jit(solution)/shard_map/ppermute | solution.py:25
  254.8 18.2 %collective-permute-start.4 = (f32[2,4,128,256]{3,2,1,0:T(8,128)S(1)}, f32[2,4,128,256]{3,2,1,0:T(8,128)S(1)}, u32[]{:S(2)}, u32[]{:S(2)}) collective-permute-start(f32[2,4,128,256]{3,2,1,0:T(8,128)S(1)} %get-tuple-element.20), channel_id=1, source_target_pairs={{0,4},{4,8},{8,12},{12,16},{16,20},{20,24},{24,28},{28,32},{32,36}... | collective-permute-start | bytes 3145736 | tf_op jit(solution)/shard_map/ppermute | solution.py:22
  273.1 6.9 %collective-permute-start.7 = (f32[2,16,4,256]{3,2,1,0:T(4,128)S(1)}, f32[2,16,4,256]{3,2,1,0:T(4,128)S(1)}, u32[]{:S(2)}, u32[]{:S(2)}) collective-permute-start(f32[2,16,4,256]{3,2,1,0:T(4,128)S(1)} %get-tuple-element.9), channel_id=1, source_target_pairs={{1,0},{2,1},{3,2},{5,4},{6,5},{7,6},{9,8},{10,9},{11,10},{13,12},{... | collective-permute-start | bytes 393224 | tf_op jit(solution)/shard_map/ppermute | solution.py:25
  277.2 6.9 %collective-permute-start.6 = (f32[2,16,4,256]{3,2,1,0:T(4,128)S(1)}, f32[2,16,4,256]{3,2,1,0:T(4,128)S(1)}, u32[]{:S(2)}, u32[]{:S(2)}) collective-permute-start(f32[2,16,4,256]{3,2,1,0:T(4,128)S(1)} %get-tuple-element.8), channel_id=1, source_target_pairs={{0,1},{1,2},{2,3},{4,5},{5,6},{6,7},{8,9},{9,10},{10,11},{12,13},{... | collective-permute-start | bytes 393224 | tf_op jit(solution)/shard_map/ppermute | solution.py:22

commit v2 on v0

v2 whole, which is shorter than its diff:
```python
import jax
import jax.numpy as jnp
from jax import lax
from jax.experimental import pallas as pl
from jax.experimental.pallas import tpu as pltpu
from jax.sharding import PartitionSpec as P

SWEEPS = 4
CAP = 12
SLOT = 16
DEVS = 128
WALK = 37
scale = 1.0 / 6.25
coupling = 0.5
F32 = jnp.float32
BF16 = jnp.bfloat16
ROWS = (((1,), (0,)), ((), ()))
BOTH = (((1,), (1,)), ((), ()))
DIRS = tuple((dz, dy) for dz in (-1, 0, 1) for dy in (-1, 0, 1) if (dz, dy) != (0, 0))


def split(value):
    high = value.astype(BF16)
    return high, (value - high.astype(F32)).astype(BF16)


def dot1(a, b, dims=ROWS):
    return lax.dot_general(a, b, dims, preferred_element_type=F32)


def dot3(a, b, dims=ROWS):
    ah, al = split(a)
    bh, bl = split(b)
    return dot1(ah, bh, dims) + (dot1(ah, bl, dims) + dot1(al, bh, dims))


def kernel(
    volt, pot, trans, cond, inv, par, tgt, plc, volt_out, pot_out,
    ohc, ohp, oht, gmat, amat, ymat, coef, pt, zmat, lt, grid, sc0, se0, cnt,
    snd1, rcv1, snd2, rcv2, snd3, rcv3, snd4, rcv4,
    f0, f1, r1, r2, xa, xb,
    a2a_send, a2a_recv, halo_send, halo_recv,
):
    slab = lax.axis_index("slab")
    row = lax.axis_index("row")
    me = slab * 4 + row
    depth = pot.shape[0]
    lines = pot.shape[1]
    cells = volt.shape[1]
    half = depth * lines

    def walk(step):
        d = lax.rem(me + step * WALK, DEVS)
        return d, {"slab": lax.div(d, 4), "row": lax.rem(d, 4)}

    barrier = pltpu.get_barrier_semaphore()

    def greet(step, carry):
        _, where = walk(step)
        pl.semaphore_signal(barrier, inc=1, device_id=where)
        return carry

    for ref in (f0, f1, r1, r2):
        @pl.when(slab == 0)
        def _():
            ref[0:SWEEPS] = jnp.zeros((SWEEPS,) + ref.shape[1:], F32)

        @pl.when(slab == 31)
        def _():
            ref[depth + SWEEPS:] = jnp.zeros((SWEEPS,) + ref.shape[1:], F32)

        @pl.when(row == 0)
        def _():
            ref[:, 0:8] = jnp.zeros((ref.shape[0], 8, ref.shape[2]), F32)

        @pl.when(row == 3)
        def _():
            ref[:, lines + 8:] = jnp.zeros((ref.shape[0], 8, ref.shape[2]), F32)

    lax.fori_loop(1, DEVS, greet, 0)

    f0[SWEEPS:SWEEPS + depth, 8:8 + lines] = pot[...]

    owner = tgt[...]
    place = plc[...]
    own = (owner == lax.broadcasted_iota(jnp.int32, (DEVS, cells), 0)).astype(F32)
    ownb = own.astype(BF16)
    earlier = (
        lax.broadcasted_iota(jnp.int32, (cells, cells), 0)
        < lax.broadcasted_iota(jnp.int32, (cells, cells), 1)
    ).astype(F32).astype(BF16)
    before = dot1(ownb, earlier)
    order = jnp.sum(before * own, axis=0, keepdims=True)
    for k in range(CAP):
        ohc[k * DEVS:(k + 1) * DEVS, :] = (own * (order == float(k)).astype(F32)).astype(BF16)
    spot = lax.rem(place, 2) * half + lax.div(place, 2) + 1
    ranks = lax.broadcasted_iota(jnp.int32, (DEVS, cells), 0).astype(F32)
    here = (ranks == order).astype(F32)
    upper = lax.div(spot, 16).astype(F32)
    lower = lax.rem(spot, 16).astype(F32)
    table = 16.0 * dot1(ownb, (here * upper).astype(BF16), BOTH) + dot1(
        ownb, (here * lower).astype(BF16), BOTH
    )
    snd1[pl.ds(CAP, DEVS, stride=SLOT), :] = table

    for k in range(8):
        unit = (
            lax.broadcasted_iota(jnp.int32, (64, 512), 0) + 64 * k
            == lax.broadcasted_iota(jnp.int32, (64, 512), 1)
        ).astype(F32)
        for earlier_block in range(k):
            above = amat[64 * earlier_block:64 * (earlier_block + 1), :]
            unit = unit + jnp.where(
                par[0:1, k - 1:k] == earlier_block, coupling * above, jnp.zeros_like(above)
            )
        amat[64 * k:64 * (k + 1), :] = lax.dot_general(
            inv[k], unit, ROWS, precision=lax.Precision.HIGHEST, preferred_element_type=F32
        )
    weighted = trans[...] * cond[...]
    back = dot3(weighted, amat[...])
    back2 = dot3(back, amat[...])
    cmat = dot3(back - weighted, trans[...], BOTH)
    emat = dot3(back2, trans[...], BOTH)
    coef[0:128, :] = cmat
    coef[128:256, :] = emat

    def to_slots(hot, parts, snd):
        for group in range(CAP // 4):
            got = dot1(hot[group * 512:(group + 1) * 512, :], parts[...])
            got = got[:, 0:128] + got[:, 128:256]
            for k in range(4):
                snd[pl.ds(group * 4 + k, DEVS, stride=SLOT), :] = got[k * 128:(k + 1) * 128]

    def fill(weights, snd):
        made = dot3(weights, volt[...])
        high, low = split(jnp.transpose(made))
        pt[:, 0:128] = high
        pt[:, 128:256] = low
        to_slots(ohc, pt, snd)

    def send_all(number, snd, rcv, rows):
        def send(step, carry):
            d, where = walk(step)
            pltpu.make_async_remote_copy(
                src_ref=snd.at[pl.ds(pl.multiple_of(d * SLOT, SLOT), rows)],
                dst_ref=rcv.at[pl.ds(pl.multiple_of(me * SLOT, SLOT), rows)],
                send_sem=a2a_send.at[number],
                recv_sem=a2a_recv.at[number],
                device_id=where,
            ).start()
            return carry

        lax.fori_loop(1, DEVS, send, 0)
        mine = pl.ds(pl.multiple_of(me * SLOT, SLOT), SLOT)
        rcv[mine, :] = snd[mine, :]

    def arrived(number, rcv, rows):
        total = pl.ds(0, (DEVS - 1) * rows)
        pltpu.make_async_copy(rcv.at[total], rcv.at[total], a2a_recv.at[number]).wait()

    def departed(number, snd, rows):
        total = pl.ds(0, (DEVS - 1) * rows)
        pltpu.make_async_copy(snd.at[total], snd.at[total], a2a_send.at[number]).wait()

    def span(shift, first, count, width, low, wide):
        if shift == 0:
            return pl.ds(first, count), pl.ds(first, count)
        if shift < 0:
            return pl.ds(first, wide), pl.ds(first + count, wide)
        return pl.ds(first + count - wide, wide), pl.ds(first - wide, wide)

    def halo(number, ref, planes, act):
        for spot_of, (dz, dy) in enumerate(DIRS):
            zs, zd = span(dz, SWEEPS, depth, None, None, planes)
            ys, yd = span(dy, 8, lines, None, None, 8)
            copy = pltpu.make_async_remote_copy(
                src_ref=ref.at[zs, ys],
                dst_ref=ref.at[zd, yd],
                send_sem=halo_send.at[number * 8 + spot_of],
                recv_sem=halo_recv.at[number * 8 + spot_of],
                device_id={"slab": slab + dz, "row": row + dy},
            )
            to = (slab + dz >= 0) & (slab + dz <= 31) & (row + dy >= 0) & (row + dy <= 3)
            came = (slab - dz >= 0) & (slab - dz <= 31) & (row - dy >= 0) & (row - dy <= 3)
            if act == "start":
                @pl.when(to)
                def _():
                    copy.start()
            elif act == "recv":
                @pl.when(came)
                def _():
                    copy.wait_recv()
            else:
                @pl.when(to)
                def _():
                    copy.wait_send()

    fill(back, snd1)

    pl.semaphore_wait(barrier, DEVS - 1)
    send_all(0, snd1, rcv1, CAP + 1)
    halo(0, f0, SWEEPS, "start")
    fill(back2, snd2)

    grid[0:half, :] = pot[:, :, 0:128].reshape(half, 128)
    grid[half:, :] = pot[:, :, 128:256].reshape(half, 128)
    for q in range(4):
        rows_of = pl.ds(q * 512, 512)
        part = grid[rows_of, :]
        sc0[rows_of, :] = dot3(part, coef[0:128, :], BOTH)
        se0[rows_of, :] = dot3(part, coef[128:256, :], BOTH)
    first = dot3(amat[...], trans[...], BOTH)
    second = dot3(amat[...], first)
    ymat[...] = dot3(amat[...], volt[...])
    ymat[...] = dot3(amat[...], ymat[...])

    def rows_in(rcv):
        for k in range(CAP):
            high, low = split(rcv[pl.ds(k, DEVS, stride=SLOT), :])
            zmat[k * DEVS:(k + 1) * DEVS, 0:128] = high
            zmat[k * DEVS:(k + 1) * DEVS, 128:256] = low

    def place_rows(ref, q, value):
        z = SWEEPS + (q % 2) * 4
        x = (q // 2) * 128
        ref[z:z + 4, 8:8 + lines, x:x + 128] = value.reshape(4, lines, 128)

    arrived(0, rcv1, CAP + 1)
    asked = rcv1[pl.ds(CAP, DEVS, stride=SLOT), :] - 1.0
    asked_t = jnp.transpose(asked)
    rows_in(rcv1)
    ones = jnp.ones((128, 128), BF16)
    for q in range(4):
        rows_of = pl.ds(q * 512, 512)
        spots = (lax.broadcasted_iota(jnp.int32, (512, 128), 0) + q * 512).astype(F32)
        many = jnp.zeros((512, 128), F32)
        for k in range(CAP):
            hit = (asked_t[k:k + 1, :] == spots).astype(F32)
            many = many + hit
            ohp[rows_of, k * 128:(k + 1) * 128] = hit.astype(BF16)
        count = dot1(many.astype(BF16), ones)
        cnt[rows_of, :] = count
        got = dot1(ohp[rows_of, :], zmat[...])
        place_rows(r1, q, got[:, 0:128] + got[:, 128:256] + count * sc0[rows_of, :])
    halo(1, r1, 3, "start")
    send_all(1, snd2, rcv2, CAP)
    for q in range(4):
        spots = (lax.broadcasted_iota(jnp.int32, (128, 512), 1) + q * 512).astype(F32)
        for k in range(CAP):
            hit = (asked[:, k:k + 1] == spots).astype(F32)
            oht[k * 128:(k + 1) * 128, q * 512:(q + 1) * 512] = hit.astype(BF16)

    def gather(snd):
        high, low = split(grid[...])
        gmat[:, 0:128] = high
        gmat[:, 128:256] = low
        to_slots(oht, gmat, snd)

    gather(snd3)
    send_all(2, snd3, rcv3, CAP)

    rowsy = lax.broadcasted_iota(jnp.int32, (lines + 16, 256), 0) + (row * lines - 8)
    inside = ((rowsy >= 0) & (rowsy < 4 * lines)).astype(F32) * scale
    lanes = lax.broadcasted_iota(jnp.int32, (lines + 16, 256), 1)

    def sweep(number, src, feed, dst, last):
        def plane(z, carry):
            mid = src[z]
            total = src[z - 1] + src[z + 1] + feed[z]
            total = total + pltpu.roll(mid, 1, 0) + pltpu.roll(mid, lines + 15, 0)
            total = total + jnp.where(lanes == 0, 0.0, pltpu.roll(mid, 1, 1))
            total = total + jnp.where(lanes == 255, 0.0, pltpu.roll(mid, 255, 1))
            at = slab * depth - SWEEPS + z
            held = ((at >= 0) & (at < 32 * depth)).astype(F32)
            value = total * (inside * held)
            if last == "grid":
                dst[z, 8:8 + lines] = value[8:8 + lines]
            elif last == "out":
                dst[z - SWEEPS] = value[8:8 + lines]
            else:
                dst[z] = value
            return carry

        lax.fori_loop(number, depth + 2 * SWEEPS - number, plane, 0)

    halo(0, f0, SWEEPS, "recv")
    halo(1, r1, 3, "recv")
    sweep(1, f0, r1, xa, "")
    sweep(2, xa, r1, xb, "")
    sweep(3, xb, r1, xa, "")
    sweep(4, xa, r1, f1, "grid")
    halo(2, f1, SWEEPS, "start")
    for z in range(depth):
        grid[z * lines:(z + 1) * lines, :] = f1[SWEEPS + z, 8:8 + lines, 0:128]
        grid[half + z * lines:half + (z + 1) * lines, :] = f1[SWEEPS + z, 8:8 + lines, 128:256]
    gather(snd4)
    send_all(3, snd4, rcv4, CAP)

    arrived(1, rcv2, CAP)
    rows_in(rcv2)
    for q in range(4):
        rows_of = pl.ds(q * 512, 512)
        got = dot1(ohp[rows_of, :], zmat[...])
        more = se0[rows_of, :] + dot3(grid[rows_of, :], coef[0:128, :], BOTH)
        place_rows(r2, q, got[:, 0:128] + got[:, 128:256] + cnt[rows_of, :] * more)
    halo(3, r2, 3, "start")

    def bring(number, rcv, weights):
        arrived(number, rcv, CAP)
        for k in range(CAP):
            high, low = split(jnp.transpose(rcv[pl.ds(k, DEVS, stride=SLOT), :]))
            lt[0:128, k * 128:(k + 1) * 128] = high
            lt[128:256, k * 128:(k + 1) * 128] = low
        got = dot1(lt[...], ohc[...])
        return dot3(weights, got[0:128, :] + got[128:256, :])

    ymat[...] = ymat[...] + bring(2, rcv3, second)
    halo(2, f1, SWEEPS, "recv")
    halo(3, r2, 3, "recv")
    sweep(1, f1, r2, xa, "")
    sweep(2, xa, r2, xb, "")
    sweep(3, xb, r2, xa, "")
    sweep(4, xa, r2, pot_out, "out")
    volt_out[...] = ymat[...] + bring(3, rcv4, first)
    departed(0, snd1, CAP + 1)
    departed(1, snd2, CAP)
    departed(2, snd3, CAP)
    departed(3, snd4, CAP)
    halo(0, f0, SWEEPS, "sent")
    halo(1, r1, 3, "sent")
    halo(2, f1, SWEEPS, "sent")
    halo(3, r2, 3, "sent")


def shards(voltage, potential, transfer, conductance, inverses, parents, target, place):
    cells = voltage.shape[1]
    depth, lines, wide = potential.shape
    tall = (depth + 2 * SWEEPS, lines + 16, wide)
    vmem = pl.BlockSpec(memory_space=pltpu.VMEM)
    block = pltpu.VMEM((DEVS * SLOT, 128), F32)
    return pl.pallas_call(
        kernel,
        out_shape=(
            jax.ShapeDtypeStruct(voltage.shape, F32),
            jax.ShapeDtypeStruct(potential.shape, F32),
        ),
        in_specs=[vmem] * 8,
        out_specs=(vmem, vmem),
        scratch_shapes=[
            pltpu.VMEM((CAP * DEVS, cells), BF16),
            pltpu.VMEM((depth * lines * 2, CAP * DEVS), BF16),
            pltpu.VMEM((CAP * DEVS, depth * lines * 2), BF16),
            pltpu.VMEM((depth * lines * 2, 256), BF16),
            pltpu.VMEM((512, 512), F32),
            pltpu.VMEM((512, cells), F32),
            pltpu.VMEM((256, 128), F32),
            pltpu.VMEM((cells, 256), BF16),
            pltpu.VMEM((CAP * DEVS, 256), BF16),
            pltpu.VMEM((256, CAP * DEVS), BF16),
            pltpu.VMEM((depth * lines * 2, 128), F32),
            pltpu.VMEM((depth * lines * 2, 128), F32),
            pltpu.VMEM((depth * lines * 2, 128), F32),
            pltpu.VMEM((depth * lines * 2, 128), F32),
        ]
        + [block] * 8
        + [pltpu.VMEM(tall, F32)] * 6
        + [
            pltpu.SemaphoreType.DMA((4,)),
            pltpu.SemaphoreType.DMA((4,)),
            pltpu.SemaphoreType.DMA((32,)),
            pltpu.SemaphoreType.DMA((32,)),
        ],
        compiler_params=pltpu.CompilerParams(
            collective_id=0, has_side_effects=True, vmem_limit_bytes=60 * 1024 * 1024
        ),
    )(
        voltage, potential, transfer, conductance.reshape(1, -1), inverses, parents.reshape(1, -1),
        target.reshape(1, -1), place.reshape(1, -1),
    )


def solution(mesh):
    return jax.shard_map(
        shards,
        mesh=mesh,
        in_specs=(
            P(None, ("slab", "row")),
            P("slab", "row", None),
            P(),
            P(),
            P(),
            P(),
            P(("slab", "row"), None),
            P(("slab", "row")),
        ),
        out_specs=(P(None, ("slab", "row")), P("slab", "row", None)),
        check_vma=False,
    )
```

time: 287 us -> 100 us (0.35)
  the two profiles are of different devices: /device:TPU:34 before, /device:TPU:1 now
where the time goes in v2:
time: 100 us; the launch traced here: 99.8 us
  Pallas kernels  94.2 us (94%)
  local copies, waits for them, and re-layouts  4.98 us (5%)
    pallas_call x1, Pallas kernels, shards(): pl.pallas_call(kernel, out_shape=(jax.ShapeDtypeStruct(voltage.shape, F32...  94.2 us
    unnamed x4, local copies, waits for them, and re-layouts  3.71 us

profile of v2, /device:TPU:1, one launch (start us, length us, event | category | flops | bytes accessed | tf_op | source)
XLA Modules:
  0.0 99.8 jit_solution(8735223714193979622)
XLA Ops:
  0.6 1.3 %reshape.19.plc = s32[1,768]{1,0:T(1,128)} reshape(s32[768]{0:T(1024)} %param.15) | data formatting | bytes 6144 | tf_op jit(solution)/shard_map/reshape | solution.py:378
  1.9 94.2 %shard_map.95 = (f32[512,768]{1,0:T(8,128)}, f32[8,128,256]{2,1,0:T(8,128)}) custom-call(f32[512,768]{1,0:T(8,128)} %volt.1, f32[8,128,256]{2,1,0:T(8,128)} %pot.1, f32[128,512]{1,0:T(8,128)} %trans.1, f32[1,512]{1,0:T(1,128)} %bitcast.4, f32[8,64,64]{2,1,0:T(8,128)} %inv.1, s32[1,7]{1,0:T(1,128)} %bitcast.5, s32[1,768]{1,0:T(1,128)} %bitcast.3, ...), custom_call_target="tpu_custom_call" | custom-call | tf_op jit(solution)/shard_map/pallas_call | solution.py:341
  96.1 0.0 copy-start
  96.1 2.7 %copy.12 = f32[512,768]{1,0:T(8,128)} copy(f32[512,768]{1,0:T(8,128)} %get-tuple-element.4) | data formatting | bytes 3145728
  98.9 0.0 copy-done
  98.9 1.0 copy.13
Async XLA Ops:
  96.1 2.8 %copy-start = (f32[8,128,256]{2,1,0:T(8,128)S(1)}, f32[8,128,256]{2,1,0:T(8,128)}, u32[]{:S(2)}) copy-start(f32[8,128,256]{2,1,0:T(8,128)} %get-tuple-element.5) | copy-start | bytes 3145732

commit v3 on v2

--- a/solution.py
+++ b/solution.py
@@ -16,7 +16,7 @@
 BF16 = jnp.bfloat16
 ROWS = (((1,), (0,)), ((), ()))
 BOTH = (((1,), (1,)), ((), ()))
-DIRS = tuple((dz, dy) for dz in (-1, 0, 1) for dy in (-1, 0, 1) if (dz, dy) != (0, 0))
+DIRS = ((-1, 0), (1, 0), (0, -1), (0, 1))
 
 
 def split(value):
@@ -38,7 +38,7 @@
     volt, pot, trans, cond, inv, par, tgt, plc, volt_out, pot_out,
     ohc, ohp, oht, gmat, amat, ymat, coef, pt, zmat, lt, grid, sc0, se0, cnt,
     snd1, rcv1, snd2, rcv2, snd3, rcv3, snd4, rcv4,
-    f0, f1, r1, r2, xa, xb,
+    field, feed,
     a2a_send, a2a_recv, halo_send, halo_recv,
 ):
     slab = lax.axis_index("slab")
@@ -60,26 +60,28 @@
         pl.semaphore_signal(barrier, inc=1, device_id=where)
         return carry
 
-    for ref in (f0, f1, r1, r2):
-        @pl.when(slab == 0)
-        def _():
-            ref[0:SWEEPS] = jnp.zeros((SWEEPS,) + ref.shape[1:], F32)
-
-        @pl.when(slab == 31)
-        def _():
-            ref[depth + SWEEPS:] = jnp.zeros((SWEEPS,) + ref.shape[1:], F32)
-
-        @pl.when(row == 0)
-        def _():
-            ref[:, 0:8] = jnp.zeros((ref.shape[0], 8, ref.shape[2]), F32)
-
-        @pl.when(row == 3)
-        def _():
-            ref[:, lines + 8:] = jnp.zeros((ref.shape[0], 8, ref.shape[2]), F32)
+    edge = (field.shape[0], 1) + field.shape[2:]
+    side = (field.shape[0], depth + 2, 8, field.shape[3])
+
+    @pl.when(slab == 0)
+    def _():
+        field[:, 0:1] = jnp.zeros(edge, F32)
+
+    @pl.when(slab == 31)
+    def _():
+        field[:, depth + 1:] = jnp.zeros(edge, F32)
+
+    @pl.when(row == 0)
+    def _():
+        field[:, :, 0:8] = jnp.zeros(side, F32)
+
+    @pl.when(row == 3)
+    def _():
+        field[:, :, lines + 8:] = jnp.zeros(side, F32)
 
     lax.fori_loop(1, DEVS, greet, 0)
 
-    f0[SWEEPS:SWEEPS + depth, 8:8 + lines] = pot[...]
+    field[0, 1:1 + depth, 8:8 + lines] = pot[...]
 
     owner = tgt[...]
     place = plc[...]
@@ -138,7 +140,7 @@
         pt[:, 128:256] = low
         to_slots(ohc, pt, snd)
 
-    def send_all(number, snd, rcv, rows):
+    def send_part(number, snd, rcv, rows, first, last):
         def send(step, carry):
             d, where = walk(step)
             pltpu.make_async_remote_copy(
@@ -150,9 +152,10 @@
             ).start()
             return carry
 
-        lax.fori_loop(1, DEVS, send, 0)
-        mine = pl.ds(pl.multiple_of(me * SLOT, SLOT), SLOT)
-        rcv[mine, :] = snd[mine, :]
+        lax.fori_loop(max(first * DEVS // 4, 1), last * DEVS // 4, send, 0)
+        if last == 4:
+            mine = pl.ds(pl.multiple_of(me * SLOT, SLOT), SLOT)
+            rcv[mine, :] = snd[mine, :]
 
     def arrived(number, rcv, rows):
         total = pl.ds(0, (DEVS - 1) * rows)
@@ -162,45 +165,40 @@
         total = pl.ds(0, (DEVS - 1) * rows)
         pltpu.make_async_copy(snd.at[total], snd.at[total], a2a_send.at[number]).wait()
 
-    def span(shift, first, count, width, low, wide):
-        if shift == 0:
-            return pl.ds(first, count), pl.ds(first, count)
-        if shift < 0:
-            return pl.ds(first, wide), pl.ds(first + count, wide)
-        return pl.ds(first + count - wide, wide), pl.ds(first - wide, wide)
-
-    def halo(number, ref, planes, act):
-        for spot_of, (dz, dy) in enumerate(DIRS):
-            zs, zd = span(dz, SWEEPS, depth, None, None, planes)
-            ys, yd = span(dy, 8, lines, None, None, 8)
+    def halo(number, act):
+        ref = field.at[number]
+        for at, (dz, dy) in enumerate(DIRS):
+            inner_z = pl.ds(1, depth)
+            inner_y = pl.ds(8, lines)
+            if dz:
+                src = ref.at[pl.ds(1 if dz < 0 else depth, 1), inner_y]
+                dst = ref.at[pl.ds(depth + 1 if dz < 0 else 0, 1), inner_y]
+            else:
+                src = ref.at[inner_z, pl.ds(8 if dy < 0 else lines, 8)]
+                dst = ref.at[inner_z, pl.ds(lines + 8 if dy < 0 else 0, 8)]
             copy = pltpu.make_async_remote_copy(
-                src_ref=ref.at[zs, ys],
-                dst_ref=ref.at[zd, yd],
-                send_sem=halo_send.at[number * 8 + spot_of],
-                recv_sem=halo_recv.at[number * 8 + spot_of],
+                src_ref=src,
+                dst_ref=dst,
+                send_sem=halo_send.at[number * 4 + at],
+                recv_sem=halo_recv.at[number * 4 + at],
                 device_id={"slab": slab + dz, "row": row + dy},
             )
             to = (slab + dz >= 0) & (slab + dz <= 31) & (row + dy >= 0) & (row + dy <= 3)
             came = (slab - dz >= 0) & (slab - dz <= 31) & (row - dy >= 0) & (row - dy <= 3)
             if act == "start":
-                @pl.when(to)
-                def _():
-                    copy.start()
+                pl.when(to)(copy.start)
             elif act == "recv":
-                @pl.when(came)
-                def _():
-                    copy.wait_recv()
+                pl.when(came)(copy.wait_recv)
             else:
-                @pl.when(to)
-                def _():
-                    copy.wait_send()
+                pl.when(to)(copy.wait_send)
 
     fill(back, snd1)
 
     pl.semaphore_wait(barrier, DEVS - 1)
-    send_all(0, snd1, rcv1, CAP + 1)
-    halo(0, f0, SWEEPS, "start")
+    halo(0, "start")
+    send_part(0, snd1, rcv1, CAP + 1, 0, 4)
     fill(back2, snd2)
+    send_part(1, snd2, rcv2, CAP, 0, 2)
 
     grid[0:half, :] = pot[:, :, 0:128].reshape(half, 128)
     grid[half:, :] = pot[:, :, 128:256].reshape(half, 128)
@@ -220,10 +218,10 @@
             zmat[k * DEVS:(k + 1) * DEVS, 0:128] = high
             zmat[k * DEVS:(k + 1) * DEVS, 128:256] = low
 
-    def place_rows(ref, q, value):
-        z = SWEEPS + (q % 2) * 4
+    def place_rows(number, q, value):
+        z = (q % 2) * 4
         x = (q // 2) * 128
-        ref[z:z + 4, 8:8 + lines, x:x + 128] = value.reshape(4, lines, 128)
+        feed[number, z:z + 4, :, x:x + 128] = value.reshape(4, lines, 128)
 
     arrived(0, rcv1, CAP + 1)
     asked = rcv1[pl.ds(CAP, DEVS, stride=SLOT), :] - 1.0
@@ -241,14 +239,13 @@
         count = dot1(many.astype(BF16), ones)
         cnt[rows_of, :] = count
         got = dot1(ohp[rows_of, :], zmat[...])
-        place_rows(r1, q, got[:, 0:128] + got[:, 128:256] + count * sc0[rows_of, :])
-    halo(1, r1, 3, "start")
-    send_all(1, snd2, rcv2, CAP)
-    for q in range(4):
-        spots = (lax.broadcasted_iota(jnp.int32, (128, 512), 1) + q * 512).astype(F32)
-        for k in range(CAP):
-            hit = (asked[:, k:k + 1] == spots).astype(F32)
-            oht[k * 128:(k + 1) * 128, q * 512:(q + 1) * 512] = hit.astype(BF16)
+        place_rows(0, q, got[:, 0:128] + got[:, 128:256] + count * sc0[rows_of, :])
+    def table_of_asked():
+        for q in range(4):
+            spots = (lax.broadcasted_iota(jnp.int32, (128, 512), 1) + q * 512).astype(F32)
+            for k in range(CAP):
+                hit = (asked[:, k:k + 1] == spots).astype(F32)
+                oht[k * 128:(k + 1) * 128, q * 512:(q + 1) * 512] = hit.astype(BF16)
 
     def gather(snd):
         high, low = split(grid[...])
@@ -256,54 +253,54 @@
         gmat[:, 128:256] = low
         to_slots(oht, gmat, snd)
 
-    gather(snd3)
-    send_all(2, snd3, rcv3, CAP)
-
-    rowsy = lax.broadcasted_iota(jnp.int32, (lines + 16, 256), 0) + (row * lines - 8)
-    inside = ((rowsy >= 0) & (rowsy < 4 * lines)).astype(F32) * scale
-    lanes = lax.broadcasted_iota(jnp.int32, (lines + 16, 256), 1)
-
-    def sweep(number, src, feed, dst, last):
-        def plane(z, carry):
-            mid = src[z]
-            total = src[z - 1] + src[z + 1] + feed[z]
-            total = total + pltpu.roll(mid, 1, 0) + pltpu.roll(mid, lines + 15, 0)
-            total = total + jnp.where(lanes == 0, 0.0, pltpu.roll(mid, 1, 1))
-            total = total + jnp.where(lanes == 255, 0.0, pltpu.roll(mid, 255, 1))
-            at = slab * depth - SWEEPS + z
-            held = ((at >= 0) & (at < 32 * depth)).astype(F32)
-            value = total * (inside * held)
-            if last == "grid":
-                dst[z, 8:8 + lines] = value[8:8 + lines]
-            elif last == "out":
-                dst[z - SWEEPS] = value[8:8 + lines]
-            else:
-                dst[z] = value
-            return carry
-
-        lax.fori_loop(number, depth + 2 * SWEEPS - number, plane, 0)
-
-    halo(0, f0, SWEEPS, "recv")
-    halo(1, r1, 3, "recv")
-    sweep(1, f0, r1, xa, "")
-    sweep(2, xa, r1, xb, "")
-    sweep(3, xb, r1, xa, "")
-    sweep(4, xa, r1, f1, "grid")
-    halo(2, f1, SWEEPS, "start")
-    for z in range(depth):
-        grid[z * lines:(z + 1) * lines, :] = f1[SWEEPS + z, 8:8 + lines, 0:128]
-        grid[half + z * lines:half + (z + 1) * lines, :] = f1[SWEEPS + z, 8:8 + lines, 128:256]
-    gather(snd4)
-    send_all(3, snd4, rcv4, CAP)
-
-    arrived(1, rcv2, CAP)
-    rows_in(rcv2)
-    for q in range(4):
-        rows_of = pl.ds(q * 512, 512)
-        got = dot1(ohp[rows_of, :], zmat[...])
-        more = se0[rows_of, :] + dot3(grid[rows_of, :], coef[0:128, :], BOTH)
-        place_rows(r2, q, got[:, 0:128] + got[:, 128:256] + cnt[rows_of, :] * more)
-    halo(3, r2, 3, "start")
+    lane = lax.broadcasted_iota(jnp.int32, (8, 128), 1)
+    line = lax.broadcasted_iota(jnp.int32, (8, 128), 0)
+    zero = jnp.zeros((8, 128), F32)
+    tiles = lines // 8
+
+    def sweep(number):
+        src = field.at[number]
+        last = number + 1 == 2 * SWEEPS
+
+        def tile(at_z, t, h):
+            return src[at_z, 8 * t + 8:8 * t + 16, 128 * h:128 * h + 128]
+
+        def strip(z, which):
+            for t in which:
+                left, right = tile(z, t, 0), tile(z, t, 1)
+                before_x = (jnp.where(lane == 127, zero, left), jnp.where(lane == 127, left, right))
+                after_x = (jnp.where(lane == 0, right, left), jnp.where(lane == 0, zero, right))
+                for h, mid in enumerate((left, right)):
+                    x = slice(128 * h, 128 * h + 128)
+                    total = tile(z - 1, t, h) + tile(z + 1, t, h)
+                    total = total + feed[number // SWEEPS, z - 1, 8 * t:8 * t + 8, x]
+                    total = total + (
+                        pltpu.roll(jnp.where(line == 7, tile(z, t - 1, h), mid), 1, 0)
+                        + pltpu.roll(jnp.where(line == 0, tile(z, t + 1, h), mid), 7, 0)
+                    )
+                    total = total + (
+                        pltpu.roll(before_x[h], 1, 1) + pltpu.roll(after_x[h], 127, 1)
+                    )
+                    if last:
+                        pot_out[z - 1, 8 * t:8 * t + 8, x] = total * scale
+                    else:
+                        field[number + 1, z, 8 * t + 8:8 * t + 16, x] = total * scale
+
+        def over(first, count, step, which):
+            def body(i, carry):
+                strip(first + i * step, which)
+                return carry
+
+            lax.fori_loop(0, count, body, 0)
+
+        halo(number, "recv")
+        if last:
+            over(1, depth, 1, range(tiles))
+        else:
+            over(1, 2, depth - 1, range(tiles))
+            over(2, depth - 2, 1, (0, tiles - 1))
+            halo(number + 1, "start")
+            over(2, depth - 2, 1, range(1, tiles - 1))
 
     def bring(number, rcv, weights):
         arrived(number, rcv, CAP)
@@ -314,28 +311,54 @@
         got = dot1(lt[...], ohc[...])
         return dot3(weights, got[0:128, :] + got[128:256, :])
 
+    sweep(0)
+    send_part(1, snd2, rcv2, CAP, 2, 3)
+    table_of_asked()
+    sweep(1)
+    send_part(1, snd2, rcv2, CAP, 3, 4)
+    gather(snd3)
+    sweep(2)
+    send_part(2, snd3, rcv3, CAP, 0, 1)
+    sweep(3)
+    send_part(2, snd3, rcv3, CAP, 1, 3)
+    for z in range(depth):
+        now = field[SWEEPS, 1 + z, 8:8 + lines, :]
+        grid[z * lines:(z + 1) * lines, :] = now[:, 0:128]
+        grid[half + z * lines:half + (z + 1) * lines, :] = now[:, 128:256]
+    for q in range(4):
+        rows_of = pl.ds(q * 512, 512)
+        se0[rows_of, :] = cnt[rows_of, :] * (
+            se0[rows_of, :] + dot3(grid[rows_of, :], coef[0:128, :], BOTH)
+        )
+    arrived(1, rcv2, CAP)
+    rows_in(rcv2)
+    for q in range(4):
+        rows_of = pl.ds(q * 512, 512)
+        got = dot1(ohp[rows_of, :], zmat[...])
+        place_rows(1, q, got[:, 0:128] + got[:, 128:256] + se0[rows_of, :])
+    sweep(4)
+    send_part(2, snd3, rcv3, CAP, 3, 4)
+    gather(snd4)
+    send_part(3, snd4, rcv4, CAP, 0, 1)
+    sweep(5)
+    send_part(3, snd4, rcv4, CAP, 1, 2)
+    sweep(6)
+    send_part(3, snd4, rcv4, CAP, 2, 4)
+    sweep(7)
     ymat[...] = ymat[...] + bring(2, rcv3, second)
-    halo(2, f1, SWEEPS, "recv")
-    halo(3, r2, 3, "recv")
-    sweep(1, f1, r2, xa, "")
-    sweep(2, xa, r2, xb, "")
-    sweep(3, xb, r2, xa, "")
-    sweep(4, xa, r2, pot_out, "out")
     volt_out[...] = ymat[...] + bring(3, rcv4, first)
     departed(0, snd1, CAP + 1)
     departed(1, snd2, CAP)
     departed(2, snd3, CAP)
     departed(3, snd4, CAP)
-    halo(0, f0, SWEEPS, "sent")
-    halo(1, r1, 3, "sent")
-    halo(2, f1, SWEEPS, "sent")
-    halo(3, r2, 3, "sent")
+    for number in range(2 * SWEEPS):
+        halo(number, "sent")
 
 
 def shards(voltage, potential, transfer, conductance, inverses, parents, target, place):
     cells = voltage.shape[1]
     depth, lines, wide = potential.shape
-    tall = (depth + 2 * SWEEPS, lines + 16, wide)
+    tall = (2 * SWEEPS, depth + 2, lines + 16, wide)
     vmem = pl.BlockSpec(memory_space=pltpu.VMEM)
     block = pltpu.VMEM((DEVS * SLOT, 128), F32)
     return pl.pallas_call(
@@ -363,7 +386,7 @@
             pltpu.VMEM((depth * lines * 2, 128), F32),
         ]
         + [block] * 8
-        + [pltpu.VMEM(tall, F32)] * 6
+        + [pltpu.VMEM(tall, F32), pltpu.VMEM((2, depth, lines, wide), F32)]
         + [
             pltpu.SemaphoreType.DMA((4,)),
             pltpu.SemaphoreType.DMA((4,)),

time: 100 us -> 95 us (0.950)
  Pallas kernels: 94.2 us -> 88.3 us
    pallas_call x1, Pallas kernels: 94.2 us -> 88.3 us  [shards(): pl.pallas_call(kernel, out_shape=(jax.ShapeDtypeStruct(voltage.shape, F32...]
where the time goes in v3:
time: 95 us; the launch traced here: 93.9 us
  Pallas kernels  88.3 us (93%)
  local copies, waits for them, and re-layouts  4.98 us (5%)
    pallas_call x1, Pallas kernels, shards(): pl.pallas_call(kernel, out_shape=(jax.ShapeDtypeStruct(voltage.shape, F32...  88.3 us
    unnamed x4, local copies, waits for them, and re-layouts  3.71 us

profile of v3, /device:TPU:1, one launch (start us, length us, event | category | flops | bytes accessed | tf_op | source)
XLA Modules:
  0.0 93.9 jit_solution(8795041975797669457)
XLA Ops:
  0.6 1.3 %reshape.19.plc = s32[1,768]{1,0:T(1,128)} reshape(s32[768]{0:T(1024)} %param.15) | data formatting | bytes 6144 | tf_op jit(solution)/shard_map/reshape | solution.py:401
  1.9 88.3 %shard_map.95 = (f32[512,768]{1,0:T(8,128)}, f32[8,128,256]{2,1,0:T(8,128)}) custom-call(f32[512,768]{1,0:T(8,128)} %volt.1, f32[8,128,256]{2,1,0:T(8,128)} %pot.1, f32[128,512]{1,0:T(8,128)} %trans.1, f32[1,512]{1,0:T(1,128)} %bitcast.4, f32[8,64,64]{2,1,0:T(8,128)} %inv.1, s32[1,7]{1,0:T(1,128)} %bitcast.5, s32[1,768]{1,0:T(1,128)} %bitcast.3, ...), custom_call_target="tpu_custom_call" | custom-call | tf_op jit(solution)/shard_map/pallas_call | solution.py:364
  90.2 0.0 copy-start
  90.2 2.7 %copy.12 = f32[512,768]{1,0:T(8,128)} copy(f32[512,768]{1,0:T(8,128)} %get-tuple-element.4) | data formatting | bytes 3145728
  92.9 0.0 copy-done
  92.9 1.0 %copy.13 = f32[8,128,256]{2,1,0:T(8,128)} copy(f32[8,128,256]{2,1,0:T(8,128)S(1)} %copy-done) | data formatting | bytes 2097152
Async XLA Ops:
  90.2 2.8 %copy-start = (f32[8,128,256]{2,1,0:T(8,128)S(1)}, f32[8,128,256]{2,1,0:T(8,128)}, u32[]{:S(2)}) copy-start(f32[8,128,256]{2,1,0:T(8,128)} %get-tuple-element.5) | copy-start | bytes 3145732

commit v4 on v3

--- a/solution.py
+++ b/solution.py
@@ -35,7 +35,7 @@
 
 
 def kernel(
-    volt, pot, trans, cond, inv, par, tgt, plc, volt_out, pot_out,
+    volt, pot, trans, cond, inv, par, tgt, plc, volt_out, pot_out, first_out, seen_out,
     ohc, ohp, oht, gmat, amat, ymat, coef, pt, zmat, lt, grid, sc0, se0, cnt,
     snd1, rcv1, snd2, rcv2, snd3, rcv3, snd4, rcv4,
     field, feed,
@@ -198,7 +198,7 @@
     halo(0, "start")
     send_part(0, snd1, rcv1, CAP + 1, 0, 4)
     fill(back2, snd2)
-    send_part(1, snd2, rcv2, CAP, 0, 2)
+    send_part(1, snd2, rcv2, CAP, 0, 3)
 
     grid[0:half, :] = pot[:, :, 0:128].reshape(half, 128)
     grid[half:, :] = pot[:, :, 128:256].reshape(half, 128)
@@ -302,25 +302,25 @@
             halo(number + 1, "start")
             over(2, depth - 2, 1, range(1, tiles - 1))
 
-    def bring(number, rcv, weights):
+    def bring(number, rcv):
         arrived(number, rcv, CAP)
         for k in range(CAP):
             high, low = split(jnp.transpose(rcv[pl.ds(k, DEVS, stride=SLOT), :]))
             lt[0:128, k * 128:(k + 1) * 128] = high
             lt[128:256, k * 128:(k + 1) * 128] = low
         got = dot1(lt[...], ohc[...])
-        return dot3(weights, got[0:128, :] + got[128:256, :])
+        return got[0:128, :] + got[128:256, :]
 
     sweep(0)
-    send_part(1, snd2, rcv2, CAP, 2, 3)
+    send_part(1, snd2, rcv2, CAP, 3, 4)
     table_of_asked()
+    gather(snd3)
     sweep(1)
-    send_part(1, snd2, rcv2, CAP, 3, 4)
-    gather(snd3)
+    send_part(2, snd3, rcv3, CAP, 0, 1)
     sweep(2)
-    send_part(2, snd3, rcv3, CAP, 0, 1)
+    send_part(2, snd3, rcv3, CAP, 1, 2)
     sweep(3)
-    send_part(2, snd3, rcv3, CAP, 1, 3)
+    send_part(2, snd3, rcv3, CAP, 2, 4)
     for z in range(depth):
         now = field[SWEEPS, 1 + z, 8:8 + lines, :]
         grid[z * lines:(z + 1) * lines, :] = now[:, 0:128]
@@ -337,16 +337,16 @@
         got = dot1(ohp[rows_of, :], zmat[...])
         place_rows(1, q, got[:, 0:128] + got[:, 128:256] + se0[rows_of, :])
     sweep(4)
-    send_part(2, snd3, rcv3, CAP, 3, 4)
     gather(snd4)
-    send_part(3, snd4, rcv4, CAP, 0, 1)
+    send_part(3, snd4, rcv4, CAP, 0, 2)
     sweep(5)
-    send_part(3, snd4, rcv4, CAP, 1, 2)
+    send_part(3, snd4, rcv4, CAP, 2, 3)
+    volt_out[...] = ymat[...] + dot3(second, bring(2, rcv3))
+    first_out[...] = first
     sweep(6)
-    send_part(3, snd4, rcv4, CAP, 2, 4)
+    send_part(3, snd4, rcv4, CAP, 3, 4)
     sweep(7)
-    ymat[...] = ymat[...] + bring(2, rcv3, second)
-    volt_out[...] = ymat[...] + bring(3, rcv4, first)
+    seen_out[...] = bring(3, rcv4)
     departed(0, snd1, CAP + 1)
     departed(1, snd2, CAP)
     departed(2, snd3, CAP)
@@ -355,20 +355,26 @@
         halo(number, "sent")
 
 
+def finish(held, first, seen, out):
+    out[...] = held[...] + dot3(first[...], seen[...])
+
+
 def shards(voltage, potential, transfer, conductance, inverses, parents, target, place):
     cells = voltage.shape[1]
     depth, lines, wide = potential.shape
     tall = (2 * SWEEPS, depth + 2, lines + 16, wide)
     vmem = pl.BlockSpec(memory_space=pltpu.VMEM)
     block = pltpu.VMEM((DEVS * SLOT, 128), F32)
-    return pl.pallas_call(
+    held, potential, first, seen = pl.pallas_call(
         kernel,
         out_shape=(
             jax.ShapeDtypeStruct(voltage.shape, F32),
             jax.ShapeDtypeStruct(potential.shape, F32),
+            jax.ShapeDtypeStruct((512, 128), F32),
+            jax.ShapeDtypeStruct((128, cells), F32),
         ),
         in_specs=[vmem] * 8,
-        out_specs=(vmem, vmem),
+        out_specs=(vmem,) * 4,
         scratch_shapes=[
             pltpu.VMEM((CAP * DEVS, cells), BF16),
             pltpu.VMEM((depth * lines * 2, CAP * DEVS), BF16),
@@ -400,6 +406,19 @@
         voltage, potential, transfer, conductance.reshape(1, -1), inverses, parents.reshape(1, -1),
         target.reshape(1, -1), place.reshape(1, -1),
     )
+    width = 256
+    voltage = pl.pallas_call(
+        finish,
+        grid=(cells // width,),
+        out_shape=jax.ShapeDtypeStruct(held.shape, F32),
+        in_specs=[
+            pl.BlockSpec((512, width), lambda i: (0, i)),
+            pl.BlockSpec((512, 128), lambda i: (0, 0)),
+            pl.BlockSpec((128, width), lambda i: (0, i)),
+        ],
+        out_specs=pl.BlockSpec((512, width), lambda i: (0, i)),
+    )(held, first, seen)
+    return voltage, potential
 
 
 def solution(mesh):

time: 95 us -> 95.4 us (level)
  Pallas kernels: 88.3 us -> 92.3 us
  local copies, waits for them, and re-layouts: 4.98 us -> 2.24 us
    pallas_call x0 -> x1, Pallas kernels: none -> 4.05 us  [shards(): pl.pallas_call(finish, grid=(cells // width,), out_shape=jax.ShapeDtypeSt...]
    unnamed x4 -> x3, local copies, waits for them, and re-layouts: 3.71 us -> 0.97 us
where the time goes in v4:
time: 95.4 us; the launch traced here: 95.2 us
  Pallas kernels  92.3 us (97%)
  local copies, waits for them, and re-layouts  2.24 us (2%)
    pallas_call x1, Pallas kernels, shards(): pl.pallas_call(kernel, out_shape=(jax.ShapeDtypeStruct(voltage.shape, F32...  88.3 us
    pallas_call x1, Pallas kernels, shards(): pl.pallas_call(finish, grid=(cells // width,), out_shape=jax.ShapeDtypeSt...  4.05 us

profile of v4, /device:TPU:1, one launch (start us, length us, event | category | flops | bytes accessed | tf_op | source)
XLA Modules:
  0.0 95.2 jit_solution(818450079915486181)
XLA Ops:
  0.6 1.3 %reshape.19.plc = s32[1,768]{1,0:T(1,128)} reshape(s32[768]{0:T(1024)} %param.15) | data formatting | bytes 6144 | tf_op jit(solution)/shard_map/reshape | solution.py:407
  1.9 88.3 %shard_map.95 = (f32[512,768]{1,0:T(8,128)}, f32[8,128,256]{2,1,0:T(8,128)}, f32[512,128]{1,0:T(8,128)}, f32[128,768]{1,0:T(8,128)}) custom-call(f32[512,768]{1,0:T(8,128)} %volt.1, f32[8,128,256]{2,1,0:T(8,128)} %pot.1, f32[128,512]{1,0:T(8,128)} %trans.1, f32[1,512]{1,0:T(1,128)} %bitcast.4, f32[8,64,64]{2,1,0:T(8,128)} %inv.1, s32[1,7]{1,0:T(1,128)} %bitcast.5, ...), custom_call_target="tpu_custom_call" | custom-call | tf_op jit(solution)/shard_map/pallas_call | solution.py:368
  90.2 0.0 copy-start
  90.2 4.0 %shard_map.96 = f32[512,768]{1,0:T(8,128)} custom-call(f32[512,768]{1,0:T(8,128)} %get-tuple-element.6.held, f32[512,128]{1,0:T(8,128)} %get-tuple-element.7.first, f32[128,768]{1,0:T(8,128)} %get-tuple-element.8.seen), custom_call_target="tpu_custom_call" | custom-call | tf_op jit(solution)/shard_map/pallas_call | solution.py:410
  94.2 0.0 copy-done
  94.2 1.0 %copy.11 = f32[8,128,256]{2,1,0:T(8,128)} copy(f32[8,128,256]{2,1,0:T(8,128)S(1)} %copy-done) | data formatting | bytes 2097152
Async XLA Ops:
  90.2 4.1 %copy-start = (f32[8,128,256]{2,1,0:T(8,128)S(1)}, f32[8,128,256]{2,1,0:T(8,128)}, u32[]{:S(2)}) copy-start(f32[8,128,256]{2,1,0:T(8,128)} %get-tuple-element.13) | copy-start | bytes 3145732

commit v5 on v4

--- a/solution.py
+++ b/solution.py
@@ -37,7 +37,7 @@
 def kernel(
     volt, pot, trans, cond, inv, par, tgt, plc, volt_out, pot_out, first_out, seen_out,
     ohc, ohp, oht, gmat, amat, ymat, coef, pt, zmat, lt, grid, sc0, se0, cnt,
-    snd1, rcv1, snd2, rcv2, snd3, rcv3, snd4, rcv4,
+    sndi, rcvi, snd1, rcv1, snd2, rcv2, snd3, rcv3, snd4, rcv4,
     field, feed,
     a2a_send, a2a_recv, halo_send, halo_recv,
 ):
@@ -84,7 +84,7 @@
     field[0, 1:1 + depth, 8:8 + lines] = pot[...]
 
     owner = tgt[...]
-    place = plc[...]
+    place = plc[...].reshape(1, cells)
     own = (owner == lax.broadcasted_iota(jnp.int32, (DEVS, cells), 0)).astype(F32)
     ownb = own.astype(BF16)
     earlier = (
@@ -103,7 +103,7 @@
     table = 16.0 * dot1(ownb, (here * upper).astype(BF16), BOTH) + dot1(
         ownb, (here * lower).astype(BF16), BOTH
     )
-    snd1[pl.ds(CAP, DEVS, stride=SLOT), :] = table
+    sndi[pl.ds(0, DEVS, stride=8), :] = table
 
     for k in range(8):
         unit = (
@@ -140,12 +140,12 @@
         pt[:, 128:256] = low
         to_slots(ohc, pt, snd)
 
-    def send_part(number, snd, rcv, rows, first, last):
+    def send_part(number, snd, rcv, rows, first, last, slot=SLOT):
         def send(step, carry):
             d, where = walk(step)
             pltpu.make_async_remote_copy(
-                src_ref=snd.at[pl.ds(pl.multiple_of(d * SLOT, SLOT), rows)],
-                dst_ref=rcv.at[pl.ds(pl.multiple_of(me * SLOT, SLOT), rows)],
+                src_ref=snd.at[pl.ds(pl.multiple_of(d * slot, slot), rows)],
+                dst_ref=rcv.at[pl.ds(pl.multiple_of(me * slot, slot), rows)],
                 send_sem=a2a_send.at[number],
                 recv_sem=a2a_recv.at[number],
                 device_id=where,
@@ -154,7 +154,7 @@
 
         lax.fori_loop(max(first * DEVS // 4, 1), last * DEVS // 4, send, 0)
         if last == 4:
-            mine = pl.ds(pl.multiple_of(me * SLOT, SLOT), SLOT)
+            mine = pl.ds(pl.multiple_of(me * slot, slot), slot)
             rcv[mine, :] = snd[mine, :]
 
     def arrived(number, rcv, rows):
@@ -196,7 +196,8 @@
 
     pl.semaphore_wait(barrier, DEVS - 1)
     halo(0, "start")
-    send_part(0, snd1, rcv1, CAP + 1, 0, 4)
+    send_part(4, sndi, rcvi, 1, 0, 4, 8)
+    send_part(0, snd1, rcv1, CAP, 0, 4)
     fill(back2, snd2)
     send_part(1, snd2, rcv2, CAP, 0, 3)
 
@@ -207,11 +208,6 @@
         part = grid[rows_of, :]
         sc0[rows_of, :] = dot3(part, coef[0:128, :], BOTH)
         se0[rows_of, :] = dot3(part, coef[128:256, :], BOTH)
-    first = dot3(amat[...], trans[...], BOTH)
-    second = dot3(amat[...], first)
-    ymat[...] = dot3(amat[...], volt[...])
-    ymat[...] = dot3(amat[...], ymat[...])
-
     def rows_in(rcv):
         for k in range(CAP):
             high, low = split(rcv[pl.ds(k, DEVS, stride=SLOT), :])
@@ -223,10 +219,9 @@
         x = (q // 2) * 128
         feed[number, z:z + 4, :, x:x + 128] = value.reshape(4, lines, 128)
 
-    arrived(0, rcv1, CAP + 1)
-    asked = rcv1[pl.ds(CAP, DEVS, stride=SLOT), :] - 1.0
+    arrived(4, rcvi, 1)
+    asked = rcvi[pl.ds(0, DEVS, stride=8), :] - 1.0
     asked_t = jnp.transpose(asked)
-    rows_in(rcv1)
     ones = jnp.ones((128, 128), BF16)
     for q in range(4):
         rows_of = pl.ds(q * 512, 512)
@@ -238,8 +233,8 @@
             ohp[rows_of, k * 128:(k + 1) * 128] = hit.astype(BF16)
         count = dot1(many.astype(BF16), ones)
         cnt[rows_of, :] = count
-        got = dot1(ohp[rows_of, :], zmat[...])
-        place_rows(0, q, got[:, 0:128] + got[:, 128:256] + count * sc0[rows_of, :])
+        sc0[rows_of, :] = count * sc0[rows_of, :]
+
     def table_of_asked():
         for q in range(4):
             spots = (lax.broadcasted_iota(jnp.int32, (128, 512), 1) + q * 512).astype(F32)
@@ -252,6 +247,17 @@
         gmat[:, 0:128] = high
         gmat[:, 128:256] = low
         to_slots(oht, gmat, snd)
+
+    table_of_asked()
+    gather(snd3)
+    first = dot3(amat[...], trans[...], BOTH)
+    second = dot3(amat[...], first)
+    arrived(0, rcv1, CAP)
+    rows_in(rcv1)
+    for q in range(4):
+        rows_of = pl.ds(q * 512, 512)
+        got = dot1(ohp[rows_of, :], zmat[...])
+        place_rows(0, q, got[:, 0:128] + got[:, 128:256] + sc0[rows_of, :])
 
     lane = lax.broadcasted_iota(jnp.int32, (8, 128), 1)
     line = lax.broadcasted_iota(jnp.int32, (8, 128), 0)
@@ -313,10 +319,10 @@
 
     sweep(0)
     send_part(1, snd2, rcv2, CAP, 3, 4)
-    table_of_asked()
-    gather(snd3)
+    ymat[...] = dot3(amat[...], volt[...])
     sweep(1)
     send_part(2, snd3, rcv3, CAP, 0, 1)
+    ymat[...] = dot3(amat[...], ymat[...])
     sweep(2)
     send_part(2, snd3, rcv3, CAP, 1, 2)
     sweep(3)
@@ -342,12 +348,19 @@
     sweep(5)
     send_part(3, snd4, rcv4, CAP, 2, 3)
     volt_out[...] = ymat[...] + dot3(second, bring(2, rcv3))
-    first_out[...] = first
+    high, low = split(first)
+    first_out[:, 0:128] = high
+    first_out[:, 128:256] = high
+    first_out[:, 256:384] = low
     sweep(6)
     send_part(3, snd4, rcv4, CAP, 3, 4)
     sweep(7)
-    seen_out[...] = bring(3, rcv4)
-    departed(0, snd1, CAP + 1)
+    high, low = split(bring(3, rcv4))
+    seen_out[0:128, :] = high
+    seen_out[128:256, :] = low
+    seen_out[256:384, :] = high
+    departed(0, snd1, CAP)
+    departed(4, sndi, 1)
     departed(1, snd2, CAP)
     departed(2, snd3, CAP)
     departed(3, snd4, CAP)
@@ -356,7 +369,7 @@
 
 
 def finish(held, first, seen, out):
-    out[...] = held[...] + dot3(first[...], seen[...])
+    out[...] = held[...] + dot1(first[...], seen[...])
 
 
 def shards(voltage, potential, transfer, conductance, inverses, parents, target, place):
@@ -370,8 +383,8 @@
         out_shape=(
             jax.ShapeDtypeStruct(voltage.shape, F32),
             jax.ShapeDtypeStruct(potential.shape, F32),
-            jax.ShapeDtypeStruct((512, 128), F32),
-            jax.ShapeDtypeStruct((128, cells), F32),
+            jax.ShapeDtypeStruct((512, 384), BF16),
+            jax.ShapeDtypeStruct((384, cells), BF16),
         ),
         in_specs=[vmem] * 8,
         out_specs=(vmem,) * 4,
@@ -391,11 +404,12 @@
             pltpu.VMEM((depth * lines * 2, 128), F32),
             pltpu.VMEM((depth * lines * 2, 128), F32),
         ]
+        + [pltpu.VMEM((DEVS * 8, 128), F32)] * 2
         + [block] * 8
         + [pltpu.VMEM(tall, F32), pltpu.VMEM((2, depth, lines, wide), F32)]
         + [
-            pltpu.SemaphoreType.DMA((4,)),
-            pltpu.SemaphoreType.DMA((4,)),
+            pltpu.SemaphoreType.DMA((5,)),
+            pltpu.SemaphoreType.DMA((5,)),
             pltpu.SemaphoreType.DMA((32,)),
             pltpu.SemaphoreType.DMA((32,)),
         ],
@@ -404,7 +418,7 @@
         ),
     )(
         voltage, potential, transfer, conductance.reshape(1, -1), inverses, parents.reshape(1, -1),
-        target.reshape(1, -1), place.reshape(1, -1),
+        target.reshape(1, -1), place,
     )
     width = 256
     voltage = pl.pallas_call(
@@ -413,8 +427,8 @@
         out_shape=jax.ShapeDtypeStruct(held.shape, F32),
         in_specs=[
             pl.BlockSpec((512, width), lambda i: (0, i)),
-            pl.BlockSpec((512, 128), lambda i: (0, 0)),
-            pl.BlockSpec((128, width), lambda i: (0, i)),
+            pl.BlockSpec((512, 384), lambda i: (0, 0)),
+            pl.BlockSpec((384, width), lambda i: (0, i)),
         ],
         out_specs=pl.BlockSpec((512, width), lambda i: (0, i)),
     )(held, first, seen)

time: 95.4 us -> 92.4 us (0.969); the launches traced: 95.2 us -> 91 us
  Pallas kernels: 92.3 us -> 89.3 us
  local copies, waits for them, and re-layouts: 2.24 us -> 0.97 us
    pallas_call x1, Pallas kernels: 88.3 us -> 85.2 us  [shards(): pl.pallas_call(kernel, out_shape=(jax.ShapeDtypeStruct(voltage.shape, F32...]
    reshape x1 -> x0, local copies, waits for them, and re-layouts: 1.27 us -> none  [shards(): place.reshape(1, -1)]
where the time goes in v5:
time: 92.4 us; the launch traced here: 91 us
  Pallas kernels  89.3 us (97%)
  local copies, waits for them, and re-layouts  0.97 us (1%)
    pallas_call x1, Pallas kernels, shards(): pl.pallas_call(kernel, out_shape=(jax.ShapeDtypeStruct(voltage.shape, F32...  85.2 us
    pallas_call x1, Pallas kernels, shards(): pl.pallas_call(finish, grid=(cells // width,), out_shape=jax.ShapeDtypeSt...  4.18 us

profile of v5, /device:TPU:1, one launch (start us, length us, event | category | flops | bytes accessed | tf_op | source)
XLA Modules:
  0.0 91.0 jit_solution(11512539846508052874)
XLA Ops:
  0.6 85.2 %shard_map.95 = (f32[512,768]{1,0:T(8,128)}, f32[8,128,256]{2,1,0:T(8,128)}, bf16[512,384]{1,0:T(8,128)(2,1)}, bf16[384,768]{1,0:T(8,128)(2,1)}) custom-call(f32[512,768]{1,0:T(8,128)} %volt.1, f32[8,128,256]{2,1,0:T(8,128)} %pot.1, f32[128,512]{1,0:T(8,128)} %trans.1, f32[1,512]{1,0:T(1,128)} %bitcast.4, f32[8,64,64]{2,1,0:T(8,128)} %inv.1, ...), custom_call_target="tpu_custom_call" | custom-call | tf_op jit(solution)/shard_map/pallas_call | solution.py:381
  85.8 0.0 copy-start
  85.8 4.2 %shard_map.96 = f32[512,768]{1,0:T(8,128)} custom-call(f32[512,768]{1,0:T(8,128)} %get-tuple-element.6.held, bf16[512,384]{1,0:T(8,128)(2,1)} %get-tuple-element.7.first, bf16[384,768]{1,0:T(8,128)(2,1)} %get-tuple-element.8.seen), custom_call_target="tpu_custom_call" | custom-call | tf_op jit(solution)/shard_map/pallas_call | solution.py:424
  90.0 0.0 copy-done
  90.0 1.0 %copy.11 = f32[8,128,256]{2,1,0:T(8,128)} copy(f32[8,128,256]{2,1,0:T(8,128)S(1)} %copy-done) | data formatting | bytes 2097152
Async XLA Ops:
  85.8 4.2 %copy-start = (f32[8,128,256]{2,1,0:T(8,128)S(1)}, f32[8,128,256]{2,1,0:T(8,128)}, u32[]{:S(2)}) copy-start(f32[8,128,256]{2,1,0:T(8,128)} %get-tuple-element.13) | copy-start | bytes 3145732

commit v6 on v5

--- a/solution.py
+++ b/solution.py
@@ -368,10 +368,6 @@
         halo(number, "sent")
 
 
-def finish(held, first, seen, out):
-    out[...] = held[...] + dot1(first[...], seen[...])
-
-
 def shards(voltage, potential, transfer, conductance, inverses, parents, target, place):
     cells = voltage.shape[1]
     depth, lines, wide = potential.shape
@@ -420,18 +416,7 @@
         voltage, potential, transfer, conductance.reshape(1, -1), inverses, parents.reshape(1, -1),
         target.reshape(1, -1), place,
     )
-    width = 256
-    voltage = pl.pallas_call(
-        finish,
-        grid=(cells // width,),
-        out_shape=jax.ShapeDtypeStruct(held.shape, F32),
-        in_specs=[
-            pl.BlockSpec((512, width), lambda i: (0, i)),
-            pl.BlockSpec((512, 384), lambda i: (0, 0)),
-            pl.BlockSpec((384, width), lambda i: (0, i)),
-        ],
-        out_specs=pl.BlockSpec((512, width), lambda i: (0, i)),
-    )(held, first, seen)
+    voltage = held + dot1(first, seen)
     return voltage, potential
 
 

time: 92.4 us -> 91.6 us (level)
  Pallas kernels: 89.3 us -> 85.2 us
  matrix products: 0 us -> 3.5 us
    pallas_call x1 -> x0, Pallas kernels: 4.18 us -> none  [shards(): pl.pallas_call(finish, grid=(cells // width,), out_shape=jax.ShapeDtypeSt...]
    dot_general x0 -> x1, matrix products: none -> 3.5 us  [dot1(): return lax.dot_general(a, b, dims, preferred_element_type=F32)]
where the time goes in v6:
time: 91.6 us; the launch traced here: 90.3 us
  Pallas kernels  85.2 us (93%)
  matrix products  3.5 us (4%)
  local copies, waits for them, and re-layouts  0.97 us (1%)
    pallas_call x1, Pallas kernels, shards(): pl.pallas_call(kernel, out_shape=(jax.ShapeDtypeStruct(voltage.shape, F32...  85.2 us
    dot_general x1, matrix products, dot1(): return lax.dot_general(a, b, dims, preferred_element_type=F32)  3.5 us

profile of v6, /device:TPU:1, one launch (start us, length us, event | category | flops | bytes accessed | tf_op | source)
XLA Modules:
  0.0 90.3 jit_solution(14225434279592394690)
XLA Ops:
  0.6 85.2 %shard_map.95 = (f32[512,768]{1,0:T(8,128)}, f32[8,128,256]{2,1,0:T(8,128)}, bf16[512,384]{1,0:T(8,128)(2,1)}, bf16[384,768]{1,0:T(8,128)(2,1)}) custom-call(f32[512,768]{1,0:T(8,128)} %volt.1, f32[8,128,256]{2,1,0:T(8,128)} %pot.1, f32[128,512]{1,0:T(8,128)} %trans.1, f32[1,512]{1,0:T(1,128)} %bitcast.6, f32[8,64,64]{2,1,0:T(8,128)} %inv.1, ...), custom_call_target="tpu_custom_call" | custom-call | tf_op jit(solution)/shard_map/pallas_call | solution.py:377
  85.8 0.0 copy-start
  85.8 3.5 %convolution_add_fusion = f32[512,768]{1,0:T(8,128)} fusion(f32[512,768]{1,0:T(8,128)} %get-tuple-element.6, bf16[512,384]{1,0:T(8,128)(2,1)} %get-tuple-element.7, bf16[384,768]{1,0:T(8,128)(2,1)} %get-tuple-element.8), kind=kOutput, calls=%fused_computation | convolution fusion | flops 302383104 | bytes 4128768 | tf_op jit(solution)/shard_map/dot_general | solution.py:28
  89.3 0.0 copy-done
  89.3 1.0 %copy.11 = f32[8,128,256]{2,1,0:T(8,128)} copy(f32[8,128,256]{2,1,0:T(8,128)S(1)} %copy-done) | data formatting | bytes 2097152
Async XLA Ops:
  85.8 3.5 %copy-start = (f32[8,128,256]{2,1,0:T(8,128)S(1)}, f32[8,128,256]{2,1,0:T(8,128)}, u32[]{:S(2)}) copy-start(f32[8,128,256]{2,1,0:T(8,128)} %get-tuple-element.13) | copy-start | bytes 3145732
